TPU v7x, 32 devices: a whole 2x2x4 slice. The times are simulated.
32 devices in a mesh: row: 4 (over y, x), col: 8 (over z, core).
Axes of the slice: x: 2, y: 2, z: 4, core: 2. Of those that a mesh axis runs over, the one named last changes fastest.
Arguments:
- residuals: bfloat16 [32768, 768], P(('row', 'col')), may hold values from -6 to 6
- codes: int32 [32768, 64], P(('row', 'col')), may hold values from 0 to 255
- list_ids: int32 [32768], P(('row', 'col')), may hold values from 0 to 8191, as said below
- rotation: bfloat16 [768, 768], replicated, may hold values from -0.21875 to 0.21875
- codebook: bfloat16 [256, 768], replicated, may hold values from -6 to 6
- list_fill: int32 [8192], P(('row', 'col')), may hold values from 0 to 4095
Outputs:
- list_drift: float32 [8192, 768], P(('row', 'col'))
- list_counts: int32 [8192], P(('row', 'col'))
- new_blocks: int32 [8192], P(('row', 'col'))
Inputs may be any that keep to these rules, and one draw needn't show every extreme that they name: `list_ids`: lists are grouped in blocks of 256 consecutive ids. Among the rows of one device (aligned blocks of 1024 rows), at most 96 have lists in the same block, and in every such aligned block some list block is named by exactly 96 rows.
All inputs are finite; a program needn't handle non-finite values.
Results may differ from a plain program's by a relative error of at most 0.0029.
Values may be sent and summed in bfloat16 or wider, within the bound.
No kernel may reach another device: no remote copies, remote signals or barrier semaphores. Data moves between devices by JAX's collectives and lax.ppermute only.
A program may use at most 64 MiB of HBM per device.

v0:
```python
import jax
import jax.numpy as jnp
from jax import lax
from jax.sharding import PartitionSpec as P


def decode_rows(codes, codebook):
    vec_rows, sub_count = codes.shape
    cent_count, feat_width = codebook.shape
    sub_width = feat_width // sub_count
    code_table = codebook.reshape(cent_count, sub_count, sub_width)
    block_rows = 256
    code_blocks = codes.reshape(vec_rows // block_rows, block_rows, sub_count)

    def one_block(code_block):
        picker = (
            code_block[:, :, None] == jnp.arange(cent_count, dtype=jnp.int32)[None, None, :]
        ).astype(jnp.bfloat16)
        picked = jnp.einsum("bmk,kmj->bmj", picker, code_table, preferred_element_type=jnp.float32)
        return picked.reshape(block_rows, feat_width)

    return lax.map(one_block, code_blocks).reshape(vec_rows, feat_width)


def sum_by_list(rows_in, tags_in, list_total):
    picker = (tags_in[:, None] == jnp.arange(list_total, dtype=jnp.int32)[None, :]).astype(
        jnp.bfloat16
    )
    list_sums = lax.dot_general(
        picker, rows_in, (((0,), (0,)), ((), ())), preferred_element_type=jnp.float32
    )
    counts = jnp.sum(picker, axis=0, dtype=jnp.float32)
    return (list_sums, counts)


def rank_in_block(owner_block, owner_total):
    vec_rows = owner_block.shape[0]
    picker = (owner_block[:, None] == jnp.arange(owner_total, dtype=jnp.int32)[None, :]).astype(
        jnp.bfloat16
    )
    later = (
        jnp.arange(vec_rows, dtype=jnp.int32)[:, None]
        > jnp.arange(vec_rows, dtype=jnp.int32)[None, :]
    )
    before = jnp.dot(later.astype(jnp.bfloat16), picker, preferred_element_type=jnp.float32)
    return jnp.sum(before * picker.astype(jnp.float32), axis=1).astype(jnp.int32)


def local(residuals, codes, list_ids, rotation, codebook, list_fill):
    row_count = lax.axis_size("row")
    col_count = lax.axis_size("col")
    owner_total = row_count * col_count
    vec_rows, feat_width = residuals.shape
    lists_here = list_fill.shape[0]
    slot_cap = 3 * vec_rows // owner_total
    rotated = jnp.dot(residuals, rotation, preferred_element_type=jnp.float32)
    rebuilt = decode_rows(codes, codebook)
    encode_error = (rotated - rebuilt).astype(jnp.bfloat16)
    owner_block = list_ids // lists_here
    slot_index = owner_block * slot_cap + rank_in_block(owner_block, owner_total)
    send_rows = (
        jnp.zeros((owner_total * slot_cap, feat_width), jnp.bfloat16)
        .at[slot_index]
        .set(encode_error)
    )
    send_tags = jnp.full((owner_total * slot_cap,), -1, jnp.int32).at[slot_index].set(list_ids)
    send_rows = send_rows.reshape(row_count, col_count, slot_cap, feat_width)
    send_tags = send_tags.reshape(row_count, col_count, slot_cap)
    got_rows, got_tags = (
        lax.all_to_all(
            lax.all_to_all(send_rows, "row", split_axis=0, concat_axis=0, tiled=True),
            "col",
            split_axis=1,
            concat_axis=1,
            tiled=True,
        ),
        lax.all_to_all(
            lax.all_to_all(send_tags, "row", split_axis=0, concat_axis=0, tiled=True),
            "col",
            split_axis=1,
            concat_axis=1,
            tiled=True,
        ),
    )
    got_rows = got_rows.reshape(-1, feat_width)
    got_tags = got_tags.reshape(-1)
    list_base = (lax.axis_index("row") * col_count + lax.axis_index("col")) * lists_here
    local_index = jnp.where(got_tags >= 0, got_tags - list_base, -1)
    list_sums, counts = sum_by_list(got_rows, local_index, lists_here)
    list_counts = counts.astype(jnp.int32)
    divisor = jnp.maximum(list_counts, 1).astype(jnp.float32)
    list_drift = list_sums / divisor[:, None]
    new_blocks = (list_fill + list_counts + 127) // 128 - (list_fill + 127) // 128
    return (list_drift, list_counts, new_blocks)


def solution(mesh):
    placed = (
        P(("row", "col"), None),
        P(("row", "col"), None),
        P(("row", "col")),
        P(),
        P(),
        P(("row", "col")),
    )
    return jax.shard_map(
        local,
        mesh=mesh,
        in_specs=placed,
        out_specs=(P(("row", "col"), None), P(("row", "col")), P(("row", "col"))),
        check_vma=False,
    )
```

profile of v0, /device:TPU:0, one launch (start us, length us, event | category | flops | bytes accessed | tf_op | source)
XLA Modules:
  0.0 245.6 jit_solution(13785492173893013077)
XLA Ops:
  2.7 4.5 %scatter_custom_fusion = s32[3072]{0:T(1024)S(1)} fusion(s32[1024]{0:T(1024)S(1)} %compare_select_fusion, s32[1024]{0:T(1024)} %param.10, s32[]{:T(128)} %constant.57.clone.1), kind=kCustom, calls=%fused_computation.32 | custom fusion | bytes 12800 | tf_op jit(solution)/shard_map/scatter | solution.py:66
  7.9 5.2 %all-to-all-start = ((s32[4,8,96]{2,1,0:T(8,128)}), s32[4,8,96]{2,1,0:T(8,128)S(1)}, u32[]{:S(2)}, u32[]{:S(2)}) async-start(s32[4,8,96]{2,1,0:T(8,128)} %reshape.51), calls=%async_computation | async-start | bytes 32768 | tf_op jit(solution)/shard_map/all_to_all | solution.py:78
  13.1 1.8 reshape.52
  14.8 1.2 copy.26
  16.9 32.8 %while.10 = (s32[]{:T(128)}, f32[4,256,768]{2,1,0:T(8,128)}, s32[4,256,64]{1,0,2:T(4,128)}, bf16[256,64,12]{0,2,1:T(8,128)(2,1)}, s32[]{:T(128)}) while((s32[]{:T(128)}, f32[4,256,768]{2,1,0:T(8,128)}, s32[4,256,64]{1,0,2:T(4,128)}, bf16[256,64,12]{0,2,1:T(8,128)(2,1)}, s32[]{:T(128)}) %tuple.27), condition=%wide.region_3.4_spmd, body=%wide.region_2.3_spmd.sunk | while | flops 104857600 | bytes 6225997 | solution.py:22
  16.9 1.0 constant_dynamic-slice_fusion.2
  17.9 5.9 %fusion.27 = f32[256,64,12]{0,2,1:T(8,128)S(1)} fusion(bf16[256,64,12]{0,2,1:T(8,128)(2,1)} %get-tuple-element.90, s32[256,64]{0,1:T(8,128)S(1)} %bitcast.29), kind=kOutput, calls=%fused_computation.5.clone.1 | convolution fusion | flops 104857600 | bytes 1245184 | tf_op jit(solution)/shard_map/while/body/eval_jaxpr/bmk,kmj->bmj/dot_general | solution.py:19
  25.1 1.0 constant_dynamic-slice_fusion.2
  26.1 5.9 %fusion.27 = f32[256,64,12]{0,2,1:T(8,128)S(1)} fusion(bf16[256,64,12]{0,2,1:T(8,128)(2,1)} %get-tuple-element.90, s32[256,64]{0,1:T(8,128)S(1)} %bitcast.29), kind=kOutput, calls=%fused_computation.5.clone.1 | convolution fusion | flops 104857600 | bytes 1245184 | tf_op jit(solution)/shard_map/while/body/eval_jaxpr/bmk,kmj->bmj/dot_general | solution.py:19
  33.3 1.0 constant_dynamic-slice_fusion.2
  34.3 5.9 %fusion.27 = f32[256,64,12]{0,2,1:T(8,128)S(1)} fusion(bf16[256,64,12]{0,2,1:T(8,128)(2,1)} %get-tuple-element.90, s32[256,64]{0,1:T(8,128)S(1)} %bitcast.29), kind=kOutput, calls=%fused_computation.5.clone.1 | convolution fusion | flops 104857600 | bytes 1245184 | tf_op jit(solution)/shard_map/while/body/eval_jaxpr/bmk,kmj->bmj/dot_general | solution.py:19
  41.5 1.0 constant_dynamic-slice_fusion.2
  42.5 5.9 %fusion.27 = f32[256,64,12]{0,2,1:T(8,128)S(1)} fusion(bf16[256,64,12]{0,2,1:T(8,128)(2,1)} %get-tuple-element.90, s32[256,64]{0,1:T(8,128)S(1)} %bitcast.29), kind=kOutput, calls=%fused_computation.5.clone.1 | convolution fusion | flops 104857600 | bytes 1245184 | tf_op jit(solution)/shard_map/while/body/eval_jaxpr/bmk,kmj->bmj/dot_general | solution.py:19
  49.7 3.6 %fusion.4 = bf16[1024,768]{1,0:T(8,128)(2,1)S(1)} fusion(f32[4,256,768]{2,1,0:T(8,128)} %get-tuple-element.25, bf16[1024,768]{1,0:T(8,128)(2,1)S(1)} %copy-done, bf16[768,768]{1,0:T(8,128)(2,1)} %param.11), kind=kOutput, calls=%fused_computation.12 | convolution fusion | flops 1209532416 | bytes 7471104 | tf_op jit(solution)/shard_map/dot_general | solution.py:56
  53.3 8.2 %scatter_custom_fusion.1 = bf16[3072,768]{1,0:T(8,128)(2,1)} fusion(s32[1024]{0:T(1024)S(1)} %compare_select_fusion, bf16[1024,768]{1,0:T(8,128)(2,1)S(1)} %fusion.4, bf16[]{:T(256)} %constant.68.clone.1), kind=kCustom, calls=%fused_computation.17 | custom fusion | bytes 4718594 | tf_op jit(solution)/shard_map/scatter | solution.py:64
  61.5 4.9 %all-to-all-start.2 = ((bf16[4,8,96,768]{3,2,1,0:T(8,128)(2,1)}), bf16[4,8,96,768]{3,2,1,0:T(8,128)(2,1)}, u32[]{:S(2)}, u32[]{:S(2)}) async-start(bf16[4,8,96,768]{3,2,1,0:T(8,128)(2,1)} %bitcast.27), calls=%async_computation.2 | async-start | bytes 9437184 | tf_op jit(solution)/shard_map/all_to_all | solution.py:71
  67.1 52.4 %all-to-all-done.2 = bf16[4,8,96,768]{3,2,1,0:T(8,128)(2,1)} async-done(((bf16[4,8,96,768]{3,2,1,0:T(8,128)(2,1)}), bf16[4,8,96,768]{3,2,1,0:T(8,128)(2,1)}, u32[]{:S(2)}, u32[]{:S(2)}) %all-to-all-start.2) | async-done | bytes 4718624 | tf_op jit(solution)/shard_map/all_to_all | solution.py:71
  119.5 4.9 %all-to-all-start.1 = ((s32[4,8,96]{2,0,1:T(4,128)}), s32[4,8,96]{2,0,1:T(4,128)S(1)}, u32[]{:S(2)}, u32[]{:S(2)}) async-start(s32[4,8,96]{2,0,1:T(4,128)} %copy.24), calls=%async_computation.1 | async-start | bytes 32768 | tf_op jit(solution)/shard_map/all_to_all | solution.py:77
  124.4 4.9 %copy.29 = bf16[4,8,96,768]{3,2,0,1:T(8,128)(2,1)} copy(bf16[4,8,96,768]{3,2,1,0:T(8,128)(2,1)} %all-to-all-done.2) | data formatting | bytes 9437184 | tf_op jit(solution)/shard_map/all_to_all | solution.py:71
  130.0 4.8 %all-to-all-start.3 = ((bf16[4,8,96,768]{3,2,0,1:T(8,128)(2,1)}), bf16[4,8,96,768]{3,2,0,1:T(8,128)(2,1)}, u32[]{:S(2)}, u32[]{:S(2)}) async-start(bf16[4,8,96,768]{3,2,0,1:T(8,128)(2,1)} %copy.29), calls=%async_computation.3 | async-start | bytes 9437184 | tf_op jit(solution)/shard_map/all_to_all | solution.py:70
  134.9 1.4 convert_reduce_fusion
  136.9 103.0 %all-to-all-done.3 = bf16[4,8,96,768]{3,2,0,1:T(8,128)(2,1)} async-done(((bf16[4,8,96,768]{3,2,0,1:T(8,128)(2,1)}), bf16[4,8,96,768]{3,2,0,1:T(8,128)(2,1)}, u32[]{:S(2)}, u32[]{:S(2)}) %all-to-all-start.3) | async-done | bytes 4718624 | tf_op jit(solution)/shard_map/all_to_all | solution.py:70
  239.9 2.7 %copy.30 = bf16[4,8,96,768]{3,2,1,0:T(8,128)(2,1)S(1)} copy(bf16[4,8,96,768]{3,2,0,1:T(8,128)(2,1)} %all-to-all-done.3) | data formatting | bytes 9437184 | tf_op jit(solution)/shard_map/all_to_all | solution.py:70
  242.6 3.0 %fusion.10 = f32[256,768]{1,0:T(8,128)} fusion(bf16[3072,768]{1,0:T(8,128)(2,1)S(1)} %bitcast.28, s32[3072]{0:T(1024)S(1)} %select_n.31, f32[256]{0:T(256)S(1)} %maximum_convert_fusion), kind=kOutput, calls=%fused_computation.20 | convolution fusion | flops 1208942592 | bytes 5518336 | tf_op jit(solution)/shard_map/dot_general | solution.py:29
  (36 shorter events, 10.9 us)
Async XLA Ops:
  0.6 49.1 %copy-start = (bf16[1024,768]{1,0:T(8,128)(2,1)S(1)}, bf16[1024,768]{1,0:T(8,128)(2,1)}, u32[]{:S(2)}) copy-start(bf16[1024,768]{1,0:T(8,128)(2,1)} %param.8) | copy-start | bytes 4718596
  7.9 53.7 %all-to-all-start = ((s32[4,8,96]{2,1,0:T(8,128)}), s32[4,8,96]{2,1,0:T(8,128)S(1)}, u32[]{:S(2)}, u32[]{:S(2)}) async-start(s32[4,8,96]{2,1,0:T(8,128)} %reshape.51), calls=%async_computation | async-start | bytes 32768 | tf_op jit(solution)/shard_map/all_to_all | solution.py:78
  61.5 58.0 %all-to-all-start.2 = ((bf16[4,8,96,768]{3,2,1,0:T(8,128)(2,1)}), bf16[4,8,96,768]{3,2,1,0:T(8,128)(2,1)}, u32[]{:S(2)}, u32[]{:S(2)}) async-start(bf16[4,8,96,768]{3,2,1,0:T(8,128)(2,1)} %bitcast.27), calls=%async_computation.2 | async-start | bytes 9437184 | tf_op jit(solution)/shard_map/all_to_all | solution.py:71
  119.5 10.5 %all-to-all-start.1 = ((s32[4,8,96]{2,0,1:T(4,128)}), s32[4,8,96]{2,0,1:T(4,128)S(1)}, u32[]{:S(2)}, u32[]{:S(2)}) async-start(s32[4,8,96]{2,0,1:T(4,128)} %copy.24), calls=%async_computation.1 | async-start | bytes 32768 | tf_op jit(solution)/shard_map/all_to_all | solution.py:77
  129.3 7.0 %copy-start.2 = (s32[256]{0:T(256)S(1)}, s32[256]{0:T(256)}, u32[]{:S(2)}) copy-start(s32[256]{0:T(256)} %param.13) | copy-start | bytes 3076
  130.0 109.8 %all-to-all-start.3 = ((bf16[4,8,96,768]{3,2,0,1:T(8,128)(2,1)}), bf16[4,8,96,768]{3,2,0,1:T(8,128)(2,1)}, u32[]{:S(2)}, u32[]{:S(2)}) async-start(bf16[4,8,96,768]{3,2,0,1:T(8,128)(2,1)} %copy.29), calls=%async_computation.3 | async-start | bytes 9437184 | tf_op jit(solution)/shard_map/all_to_all | solution.py:70
  136.9 105.7 %copy-start.1 = (s32[256]{0:T(256)}, s32[256]{0:T(256)S(1)}, u32[]{:S(2)}) copy-start(s32[256]{0:T(256)S(1)} %get-tuple-element.51) | copy-start | bytes 3076
where the time goes:
time: 247 us; the launch traced here: 246 us
  waiting for transfers between devices  156 us (63%)
  local copies, waits for them, and re-layouts  34.7 us (14%)
  matrix products  30.6 us (12%)
  starting transfers between devices  19.8 us (8%)
  other arithmetic  3.47 us (1%)
    all_to_all x1, waiting for transfers between devices, local(): lax.all_to_all(lax.all_to_all(send_rows, 'row', split_axis=0, concat_axis...  103 us
    all_to_all x1, waiting for transfers between devices, local(): lax.all_to_all(send_rows, 'row', split_axis=0, concat_axis=0, tiled=True)  52.4 us
    dot_general x4, matrix products, one_block(): jnp.einsum('bmk,kmj->bmj', picker, code_table, preferred_element_type=jnp...  23.5 us
    scatter x1, local copies, waits for them, and re-layouts, local(): send_rows = jnp.zeros((owner_total * slot_cap, feat_width), jnp.bfloat16)...  8.18 us
    all_to_all x1, starting transfers between devices, local(): lax.all_to_all(send_tags, 'row', split_axis=0, concat_axis=0, tiled=True)  5.19 us
  transfers between devices with their start and end apart: 4, of which 3 were waited for; matrix products, arithmetic and copies ran while one was open for 23% of the time, Pallas kernels for 0%

commit v1 on v0

v1 whole, which is shorter than its diff:
```python
import functools

import jax
import jax.numpy as jnp
from jax import lax
from jax.experimental import pallas as pl
from jax.experimental.pallas import tpu as pltpu
from jax.sharding import PartitionSpec as P

CHUNKS = 3
F32 = jnp.float32
BF16 = jnp.bfloat16
NT = (((1,), (1,)), ((), ()))


def up(value, step):
    return (value + step - 1) // step * step


def tag_rows(slots, width):
    return up(8 * (-(-slots // width)), 16)


def iota(shape, dim):
    return lax.broadcasted_iota(jnp.int32, shape, dim)


def hot(test):
    return jnp.where(test, 1.0, 0.0).astype(F32)


def split(total, pieces):
    while total % (128 * pieces):
        pieces -= 1
    return total // pieces


def plan_slots(ids, slots, lists_here, row_count, col_count):
    me = lax.axis_index("row")
    vecs = ids.shape[1]
    owner = ids // lists_here
    group = (owner // col_count) ^ me
    owner_col = owner % col_count
    in_list = ids % lists_here
    sub = max(8, row_count)
    member = hot(iota((sub, vecs), 0) == group)
    run = member
    lane = iota((sub, vecs), 1)
    step = 1
    while step < vecs:
        run = run + jnp.where(lane >= step, pltpu.roll(run, step, 1), 0.0)
        step *= 2
    rank = jnp.sum((run - member) * member, axis=0, keepdims=True).astype(jnp.int32)
    slot = jnp.where(rank < slots, group * slots + rank, -1)
    tags = jnp.where(
        iota((16, vecs), 0) == 0,
        (owner_col + 1).astype(F32),
        jnp.where(iota((16, vecs), 0) == 1, in_list.astype(F32), 0.0),
    )
    return slot, tags.astype(BF16)


def pack_kernel(first, slots, base, width, dsub, lists_here, row_count, col_count, *refs):
    if first:
        ids_ref, codes_ref, res_ref, rot_ref, book_ref = refs[:5]
        outs = refs[5 : 5 + row_count]
        slot_ref, ct_ref, rot_t, tab_t, err_t = refs[5 + row_count :]
        ct_ref[...] = codes_ref[...].T
        slot, tags = plan_slots(ids_ref[...], slots, lists_here, row_count, col_count)
        slot_ref[...] = jnp.broadcast_to(slot, slot_ref.shape)
    else:
        slot_ref, ct_ref, res_ref, rot_ref, book_ref = refs[:5]
        outs = refs[5 : 5 + row_count]
        rot_t, tab_t, err_t = refs[5 + row_count :]
        slot = slot_ref[0:1, :]
    vecs = res_ref.shape[0]
    cents = book_ref.shape[0]
    tab_t[...] = book_ref[...].astype(F32).T
    rot_t[...] = lax.dot_general(
        rot_ref[...], res_ref[...], (((0,), (1,)), ((), ())), preferred_element_type=F32
    )

    def lanes(block, carry):
        here = pl.ds(pl.multiple_of(block * 128, 128), 128)

        def half(row):
            first_sub = (base + row) // dsub
            last_sub = (base + row + 7) // dsub
            index = jnp.broadcast_to(ct_ref[first_sub : first_sub + 1, here], (8, 128))
            for sub in range(first_sub + 1, last_sub + 1):
                starts = sub * dsub - (base + row)
                other = jnp.broadcast_to(ct_ref[sub : sub + 1, here], (8, 128))
                index = jnp.where(iota((8, 128), 0) >= starts, other, index)
            low = index & 127
            value = None
            for part in range(0, cents, 128):
                got = jnp.take_along_axis(
                    tab_t[row : row + 8, part : part + 128], low, axis=1, mode="promise_in_bounds"
                )
                value = got if value is None else jnp.where(index >= part, got, value)
            return rot_t[row : row + 8, here] - value

        for row in range(0, width, 16):
            err_t[row : row + 16, here] = jnp.concatenate([half(row), half(row + 8)], 0).astype(BF16)
        return carry

    lax.fori_loop(0, vecs // 128, lanes, 0)
    err = err_t[...]
    for group in range(row_count):
        picker = hot(iota((slots, vecs), 0) + group * slots == slot).astype(BF16)
        rows = lax.dot_general(picker, err, NT, preferred_element_type=F32)
        outs[group][0:slots, :] = rows.astype(BF16)
        if first:
            line = lax.dot_general(tags, picker, NT, preferred_element_type=F32)[0:8, :]
            extra = outs[group].shape[0] - slots
            parts = [line[:, at : min(at + width, slots)] for at in range(0, slots, width)]
            parts = [
                part
                if part.shape[1] == width
                else jnp.concatenate([part, jnp.zeros((8, width - part.shape[1]), F32)], 1)
                for part in parts
            ]
            while len(parts) * 8 < extra:
                parts.append(jnp.zeros((8, width), F32))
            outs[group][slots:, :] = jnp.concatenate(parts, 0).astype(BF16)


def sum_kernel(first, slots, width, lists_here, row_count, zone_count, *refs):
    senders = 2 * row_count
    lane_count = senders * slots
    if first:
        got = refs[:senders]
        blocks = refs[senders : senders + zone_count]
        count_ref, key_ref, rows = refs[senders + zone_count :]
        me = lax.axis_index("col")
        zone, core = me // 2, me % 2
        keys = []
        for ref in got:
            extra = ref[slots:, :].astype(F32)
            pieces = -(-slots // width)
            line = jnp.concatenate([extra[8 * p : 8 * p + 8, :] for p in range(pieces)], 1)
            line = line[:, 0:slots].astype(jnp.int32)
            owner_col = line[0:1, :] - 1
            key = ((owner_col >> 1) ^ zone) * lists_here + line[1:2, :]
            mine = (owner_col >= 0) & ((owner_col & 1) == core)
            keys.append(jnp.where(mine, key, -1))
        for b in range(senders):
            key_ref[b : b + 1, :] = keys[b]
    else:
        key_ref = refs[0]
        got = refs[1 : 1 + senders]
        blocks = refs[1 + senders : 1 + senders + zone_count]
        rows = refs[1 + senders + zone_count]
        keys = [key_ref[b : b + 1, :] for b in range(senders)]
    for b in range(senders):
        rows[b * slots : (b + 1) * slots, :] = got[b][0:slots, :]
    whole = slots % 128 == 0
    if whole:
        keys = [jnp.concatenate(keys, 1)]
    span = lane_count if whole else slots
    for zone_at in range(zone_count):
        total = count = None
        for b, key in enumerate(keys):
            picker = hot(iota((lists_here, span), 0) + zone_at * lists_here == key)
            part = jnp.dot(
                picker.astype(BF16), rows[b * span : (b + 1) * span, :], preferred_element_type=F32
            )
            total = part if total is None else total + part
            if first:
                part = jnp.sum(picker, axis=1, keepdims=True)
                count = part if count is None else count + part
        if zone_at == 0:
            blocks[0][...] = total
        else:
            blocks[zone_at][0:lists_here, :] = total.astype(BF16)
        if first:
            eye = iota((lists_here, lists_here), 0) == iota((lists_here, lists_here), 1)
            line = jnp.sum(jnp.where(eye, count, 0.0), axis=0, keepdims=True)
            if zone_at == 0:
                count_ref[...] = jnp.broadcast_to(line, count_ref.shape)
            else:
                number = line.astype(jnp.int32)
                high = (number >> 8).astype(F32)
                low = (number & 255).astype(F32)
                shape = (16, lists_here)
                extra = jnp.where(
                    iota(shape, 0) == 0, high, jnp.where(iota(shape, 0) == 1, low, 0.0)
                )
                if width > lists_here:
                    extra = jnp.concatenate([extra, jnp.zeros((16, width - lists_here), F32)], 1)
                blocks[zone_at][lists_here:, :] = extra.astype(BF16)


def close_kernel(lists_here, width, chunks, zone_count, *refs):
    fill_ref, own_count = refs[:2]
    refs = refs[2:]
    drift_ref, count_ref, new_ref = refs[chunks * zone_count :]
    line = own_count[0:1, :]
    for at in range(1, zone_count):
        extra = refs[at][lists_here : lists_here + 16, 0:lists_here].astype(F32)
        line = line + extra[0:1, :] * 256.0 + extra[1:2, :]
    number = line.astype(jnp.int32)
    fill = fill_ref[...]
    count_ref[...] = number
    new_ref[...] = ((fill + number + 127) >> 7) - ((fill + 127) >> 7)
    eye = iota((lists_here, lists_here), 0) == iota((lists_here, lists_here), 1)
    divisor = jnp.sum(jnp.where(eye, jnp.maximum(line, 1.0), 0.0), axis=1, keepdims=True)
    for chunk in range(chunks):
        mine = refs[chunk * zone_count : (chunk + 1) * zone_count]
        total = mine[0][...]
        for at in range(1, zone_count):
            total = total + mine[at][0:lists_here, :].astype(F32)
        drift_ref[:, chunk * width : (chunk + 1) * width] = total / divisor


def vmem(count):
    return [pl.BlockSpec(memory_space=pltpu.VMEM)] * count


def call(kernel, outs, scratch, ins, name, flops, specs=None):
    size = sum(a.size * a.dtype.itemsize for a in (*ins, *outs))
    return pl.pallas_call(
        kernel,
        out_shape=outs,
        in_specs=specs or vmem(len(ins)),
        out_specs=vmem(len(outs)),
        scratch_shapes=scratch,
        grid=() if specs is None else (1,),
        name=name,
        cost_estimate=pl.CostEstimate(flops=flops, bytes_accessed=size, transcendentals=0),
        compiler_params=pltpu.CompilerParams(vmem_limit_bytes=56 * 1024 * 1024),
    )(*ins)


def shape(dims, kind):
    return jax.ShapeDtypeStruct(dims, kind)


def local(residuals, codes, list_ids, rotation, codebook, list_fill):
    row_count = lax.axis_size("row")
    col_count = lax.axis_size("col")
    vecs, feats = residuals.shape
    subs = codes.shape[1]
    dsub = feats // subs
    cents = codebook.shape[0]
    lists_here = list_fill.shape[0]
    zone_count = col_count // 2
    width = split(feats, CHUNKS)
    chunks = feats // width
    slots = 3 * vecs // row_count

    def trade(array, axis, size, mask):
        return lax.ppermute(array, axis, [(i, i ^ mask) for i in range(size)])

    ids = list_ids.reshape(1, vecs)
    fill = list_fill.reshape(1, lists_here)
    extra = tag_rows(slots, width)
    packed = []
    slot = codes_t = None
    for chunk in range(chunks):
        first = chunk == 0
        outs = [shape((slots + (extra if first else 0), width), BF16) for _ in range(row_count)]
        scratch = [
            pltpu.VMEM((width, vecs), F32),
            pltpu.VMEM((width, cents), F32),
            pltpu.VMEM((width, vecs), BF16),
        ]
        if first:
            outs += [shape((8, vecs), jnp.int32), shape((subs, vecs), jnp.int32)]
            lead = (ids, codes)
        else:
            lead = (slot, codes_t)
        ins = (*lead, residuals, rotation, codebook)

        def all_of(array):
            return pl.BlockSpec(array.shape, lambda i: (0, 0))

        def columns(array, chunk=chunk):
            return pl.BlockSpec((array.shape[0], width), lambda i: (0, chunk))

        specs = [*map(all_of, ins[:3]), columns(rotation), columns(codebook)]
        got = call(
            functools.partial(
                pack_kernel, first, slots, chunk * width, width, dsub, lists_here, row_count, col_count
            ),
            outs,
            scratch,
            ins,
            f"pack{chunk}",
            2 * vecs * width * (feats + row_count * slots),
            specs,
        )
        packed.append(got[:row_count])
        if first:
            slot, codes_t = got[row_count:]
    blocks = []
    key = count = None
    for chunk in range(chunks):
        first = chunk == 0
        mine = packed[chunk]
        got = [mine[0]] + [None] * (row_count - 1)
        for mask in sorted(range(1, row_count), key=lambda m: -bin(m).count("1")):
            got[mask] = trade(mine[mask], "row", row_count, mask)
        other = [trade(array, "col", col_count, 1) for array in got]
        outs = [shape((lists_here, width), F32)]
        outs += [
            shape((lists_here + (16 if first else 0), width), BF16) for _ in range(zone_count - 1)
        ]
        ins = [*got, *other]
        if first:
            outs += [shape((8, lists_here), F32), shape((2 * row_count, slots), jnp.int32)]
        else:
            ins = [key, *ins]
        sums = call(
            functools.partial(sum_kernel, first, slots, width, lists_here, row_count, zone_count),
            outs,
            [pltpu.VMEM((2 * row_count * slots, width), BF16)],
            ins,
            f"sum{chunk}",
            2 * zone_count * lists_here * 2 * row_count * slots * width,
        )
        if first:
            count, key = sums[zone_count:]
        blocks.append(sums[:zone_count])
    landed = []
    for chunk in range(chunks):
        mine = blocks[chunk]
        landed.append(mine[0])
        got = [None] * zone_count
        for mask in sorted(range(1, zone_count), key=lambda m: -m):
            got[mask] = trade(mine[mask], "col", col_count, 2 * mask)
        landed += got[1:]
    drift, counts, new_blocks = call(
        functools.partial(close_kernel, lists_here, width, chunks, zone_count),
        [
            shape((lists_here, feats), F32),
            shape((1, lists_here), jnp.int32),
            shape((1, lists_here), jnp.int32),
        ],
        [],
        [fill, count, *landed],
        "close",
        lists_here * feats * zone_count,
    )
    return drift, counts.reshape(-1), new_blocks.reshape(-1)


def solution(mesh):
    placed = (
        P(("row", "col"), None),
        P(("row", "col"), None),
        P(("row", "col")),
        P(),
        P(),
        P(("row", "col")),
    )
    return jax.shard_map(
        local,
        mesh=mesh,
        in_specs=placed,
        out_specs=(P(("row", "col"), None), P(("row", "col")), P(("row", "col"))),
        check_vma=False,
    )
```

time: 247 us -> 134 us (0.54)
  waiting for transfers between devices: 156 us -> 52.3 us
  Pallas kernels: 0 us -> 44 us
  matrix products: 30.6 us -> 0 us
  local copies, waits for them, and re-layouts: 34.7 us -> 4.68 us
  starting transfers between devices: 19.8 us -> 32 us
  other arithmetic: 3.47 us -> 0 us
    all_to_all x4 -> x0, waiting for transfers between devices: 156 us -> none  [the longest x1 103 us: local(): lax.all_to_all(lax.all_to_all(send_rows, 'row', split_axis=0, concat_axis...]
    ppermute x0 -> x30, waiting for transfers between devices: none -> 52.3 us  [trade(): return lax.ppermute(array, axis, [(i, i ^ mask) for i in range(size)])]
    pallas_call x0 -> x7, Pallas kernels: none -> 44 us  [call(): pl.pallas_call(kernel, out_shape=outs, in_specs=specs or vmem(len(ins)),...]
    ppermute x0 -> x30, starting transfers between devices: none -> 32 us  [trade(): return lax.ppermute(array, axis, [(i, i ^ mask) for i in range(size)])]
    dot_general x7 -> x0, matrix products: 30.6 us -> none  [the longest x4 23.5 us: one_block(): jnp.einsum('bmk,kmj->bmj', picker, code_table, preferred_element_type=jnp...]
    all_to_all x4 -> x0, starting transfers between devices: 19.8 us -> none  [the longest x1 5.19 us: local(): lax.all_to_all(send_tags, 'row', split_axis=0, concat_axis=0, tiled=True)]
    scatter x2 -> x0, local copies, waits for them, and re-layouts: 12.7 us -> none  [the longest x1 8.18 us: local(): send_rows = jnp.zeros((owner_total * slot_cap, feat_width), jnp.bfloat16)...]
    all_to_all x3 -> x0, local copies, waits for them, and re-layouts: 8.18 us -> none  [the longest x1 4.88 us: local(): lax.all_to_all(send_rows, 'row', split_axis=0, concat_axis=0, tiled=True)]
  transfers between devices with their start and end apart: 4 -> 30, of which waited for: 3 -> 9; matrix products, arithmetic and copies ran while one was open for 23% -> 0% of each run, Pallas kernels for 0% -> 19%
where the time goes in v1:
time: 134 us
  waiting for transfers between devices  52.3 us (39%)
  Pallas kernels  44 us (33%)
  starting transfers between devices  32 us (24%)
  local copies, waits for them, and re-layouts  4.68 us (3%)
    ppermute x30, waiting for transfers between devices, trade(): return lax.ppermute(array, axis, [(i, i ^ mask) for i in range(size)])  52.3 us
    pallas_call x7, Pallas kernels, call(): pl.pallas_call(kernel, out_shape=outs, in_specs=specs or vmem(len(ins)),...  44 us
    ppermute x30, starting transfers between devices, trade(): return lax.ppermute(array, axis, [(i, i ^ mask) for i in range(size)])  32 us
    unnamed x73, local copies, waits for them, and re-layouts  4.68 us
  transfers between devices with their start and end apart: 30, of which 9 were waited for; matrix products, arithmetic and copies ran while one was open for 0% of the time, Pallas kernels for 19%

profile of v1, /device:TPU:0, one launch (start us, length us, event | category | flops | bytes accessed | tf_op | source)
XLA Modules:
  0.0 133.9 jit_solution(6874934135479715327)
XLA Ops:
  0.6 1.9 %copy.9.refs_1_ = s32[1024,64]{1,0:T(8,128)} copy(s32[1024,64]{0,1:T(8,128)} %param.7) | data formatting | bytes 524288 | tf_op args[1]
  2.6 8.9 %pack0.1 = (bf16[800,256]{1,0:T(8,128)(2,1)}, bf16[800,256]{1,0:T(8,128)(2,1)}, bf16[800,256]{1,0:T(8,128)(2,1)}, bf16[800,256]{1,0:T(8,128)(2,1)}, s32[8,1024]{1,0:T(8,128)}, /*index=5*/s32[64,1024]{1,0:T(8,128)}) custom-call(s32[1,1024]{1,0:T(1,128)} %bitcast.5, s32[1024,64]{1,0:T(8,128)} %copy.9.refs_1_, bf16[1024,768]{1,0:T(8,128)(2,1)} %refs_2_.5, ...), custom_call_target="tpu_custom_call" | custom-call | flops 2013265920 | bytes 5345280 | tf_op jit(solution)/shard_map/pack0/pallas_call | solution.py:222
  11.4 6.8 %pack2.1 = (bf16[768,256]{1,0:T(8,128)(2,1)}, bf16[768,256]{1,0:T(8,128)(2,1)}, bf16[768,256]{1,0:T(8,128)(2,1)}, bf16[768,256]{1,0:T(8,128)(2,1)}) custom-call(s32[8,1024]{1,0:T(8,128)} %get-tuple-element.44.refs_0_, s32[64,1024]{1,0:T(8,128)} %get-tuple-element.45.refs_1_, bf16[1024,768]{1,0:T(8,128)(2,1)} %refs_2_.5, bf16[768,768]{1,0:T(8,128)(2,1)} %refs_3_.5, ...), custom_call_target="tpu_custom_call" | custom-call | flops 2013265920 | bytes 5013504 | tf_op jit(solution)/shard_map/pack2/pallas_call | solution.py:222
  18.3 3.0 %collective-permute-start.20 = (bf16[768,256]{1,0:T(8,128)(2,1)}, bf16[768,256]{1,0:T(8,128)(2,1)S(1)}, u32[]{:S(2)}, u32[]{:S(2)}) collective-permute-start(bf16[768,256]{1,0:T(8,128)(2,1)} %get-tuple-element.55), channel_id=1, source_target_pairs={{0,8},{8,0},{16,24},{24,16},{1,9},{9,1},{17,25},{25,17},{2,10},{10... | collective-permute-start | bytes 1179656 | tf_op jit(solution)/shard_map/ppermute | solution.py:253
  22.8 7.1 %pack1.1 = (bf16[768,256]{1,0:T(8,128)(2,1)}, bf16[768,256]{1,0:T(8,128)(2,1)}, bf16[768,256]{1,0:T(8,128)(2,1)}, bf16[768,256]{1,0:T(8,128)(2,1)}) custom-call(s32[8,1024]{1,0:T(8,128)} %get-tuple-element.44.refs_0_, s32[64,1024]{1,0:T(8,128)} %get-tuple-element.45.refs_1_, bf16[1024,768]{1,0:T(8,128)(2,1)} %refs_2_.5, bf16[768,768]{1,0:T(8,128)(2,1)} %refs_3_.5, ...), custom_call_target="tpu_custom_call" | custom-call | flops 2013265920 | bytes 5013504 | tf_op jit(solution)/shard_map/pack1/pallas_call | solution.py:222
  29.9 2.0 %collective-permute-start.10 = (bf16[768,256]{1,0:T(8,128)(2,1)}, bf16[768,256]{1,0:T(8,128)(2,1)S(1)}, u32[]{:S(2)}, u32[]{:S(2)}) collective-permute-start(bf16[768,256]{1,0:T(8,128)(2,1)} %get-tuple-element.47), channel_id=1, source_target_pairs={{0,8},{8,0},{16,24},{24,16},{1,9},{9,1},{17,25},{25,17},{2,10},{10... | collective-permute-start | bytes 1179656 | tf_op jit(solution)/shard_map/ppermute | solution.py:253
  33.4 7.5 %collective-permute-done.21.refs_3_ = bf16[768,256]{1,0:T(8,128)(2,1)S(1)} collective-permute-done((bf16[768,256]{1,0:T(8,128)(2,1)}, bf16[768,256]{1,0:T(8,128)(2,1)S(1)}, u32[]{:S(2)}, u32[]{:S(2)}) %collective-permute-start.21) | collective-permute-done | bytes 393248 | tf_op jit(solution)/shard_map/ppermute | solution.py:253
  41.5 3.4 %collective-permute-start = (bf16[800,256]{1,0:T(8,128)(2,1)S(1)}, bf16[800,256]{1,0:T(8,128)(2,1)S(1)}, u32[]{:S(2)}, u32[]{:S(2)}) collective-permute-start(bf16[800,256]{1,0:T(8,128)(2,1)S(1)} %copy-done.15), channel_id=1, source_target_pairs={{0,8},{8,0},{16,24},{24,16},{1,9},{9,1},{17,25},{25,17},{2,10},{10... | collective-permute-start | bytes 1228808 | tf_op jit(solution)/shard_map/ppermute | solution.py:253
  45.0 3.3 %collective-permute-done.10.refs_2_ = bf16[768,256]{1,0:T(8,128)(2,1)S(1)} collective-permute-done((bf16[768,256]{1,0:T(8,128)(2,1)}, bf16[768,256]{1,0:T(8,128)(2,1)S(1)}, u32[]{:S(2)}, u32[]{:S(2)}) %collective-permute-start.10) | collective-permute-done | bytes 393248 | tf_op jit(solution)/shard_map/ppermute | solution.py:253
  48.3 3.0 %collective-permute-start.2 = (bf16[800,256]{1,0:T(8,128)(2,1)S(1)}, bf16[800,256]{1,0:T(8,128)(2,1)S(1)}, u32[]{:S(2)}, u32[]{:S(2)}) collective-permute-start(bf16[800,256]{1,0:T(8,128)(2,1)S(1)} %copy-done.10), channel_id=1, source_target_pairs={{0,24},{8,16},{16,8},{24,0},{1,25},{9,17},{17,9},{25,1},{2,26},{10... | collective-permute-start | bytes 1228808 | tf_op jit(solution)/shard_map/ppermute | solution.py:253
  51.3 6.6 %collective-permute-done.11.refs_3_ = bf16[768,256]{1,0:T(8,128)(2,1)S(1)} collective-permute-done((bf16[768,256]{1,0:T(8,128)(2,1)}, bf16[768,256]{1,0:T(8,128)(2,1)S(1)}, u32[]{:S(2)}, u32[]{:S(2)}) %collective-permute-start.11) | collective-permute-done | bytes 393248 | tf_op jit(solution)/shard_map/ppermute | solution.py:253
  58.3 7.2 %collective-permute-done.refs_1_ = bf16[800,256]{1,0:T(8,128)(2,1)S(1)} collective-permute-done((bf16[800,256]{1,0:T(8,128)(2,1)S(1)}, bf16[800,256]{1,0:T(8,128)(2,1)S(1)}, u32[]{:S(2)}, u32[]{:S(2)}) %collective-permute-start) | collective-permute-done | bytes 409632 | tf_op jit(solution)/shard_map/ppermute | solution.py:253
  65.5 9.3 %collective-permute-done.1.refs_2_ = bf16[800,256]{1,0:T(8,128)(2,1)S(1)} collective-permute-done((bf16[800,256]{1,0:T(8,128)(2,1)S(1)}, bf16[800,256]{1,0:T(8,128)(2,1)S(1)}, u32[]{:S(2)}, u32[]{:S(2)}) %collective-permute-start.1) | collective-permute-done | bytes 409632 | tf_op jit(solution)/shard_map/ppermute | solution.py:253
  75.9 1.9 %collective-permute-done.25.refs_7_ = bf16[768,256]{1,0:T(8,128)(2,1)S(1)} collective-permute-done((bf16[768,256]{1,0:T(8,128)(2,1)S(1)}, bf16[768,256]{1,0:T(8,128)(2,1)S(1)}, u32[]{:S(2)}, u32[]{:S(2)}) %collective-permute-start.25) | collective-permute-done | bytes 393248 | tf_op jit(solution)/shard_map/ppermute | solution.py:253
  79.1 6.6 %sum0.1 = (f32[256,256]{1,0:T(8,128)}, bf16[272,256]{1,0:T(8,128)(2,1)}, bf16[272,256]{1,0:T(8,128)(2,1)}, bf16[272,256]{1,0:T(8,128)(2,1)}, f32[8,256]{1,0:T(8,128)}, /*index=5*/s32[8,768]{1,0:T(8,128)}) custom-call(bf16[800,256]{1,0:T(8,128)(2,1)} %get-tuple-element.34.refs_0_, bf16[800,256]{1,0:T(8,128)(2,1)} %copy-done.11, bf16[800,256]{1,0:T(8,128)(2,1)} %copy-done.12, ...), custom_call_target="tpu_custom_call" | custom-call | flops 3221225472 | bytes 3989504 | tf_op jit(solution)/shard_map/sum0/pallas_call | solution.py:222
  85.9 6.0 %sum2.1 = (f32[256,256]{1,0:T(8,128)}, bf16[256,256]{1,0:T(8,128)(2,1)}, bf16[256,256]{1,0:T(8,128)(2,1)}, bf16[256,256]{1,0:T(8,128)(2,1)}) custom-call(s32[8,768]{1,0:T(8,128)} %get-tuple-element.43.refs_0_, bf16[768,256]{1,0:T(8,128)(2,1)} %get-tuple-element.54.refs_1_, bf16[768,256]{1,0:T(8,128)(2,1)} %copy-done.22, bf16[768,256]{1,0:T(8,128)(2,1)} %copy-done.24, ...), custom_call_target="tpu_custom_call" | custom-call | flops 3221225472 | bytes 3825664 | tf_op jit(solution)/shard_map/sum2/pallas_call | solution.py:222
  93.5 2.6 %collective-permute-start.28 = (bf16[256,256]{1,0:T(8,128)(2,1)}, bf16[256,256]{1,0:T(8,128)(2,1)S(1)}, u32[]{:S(2)}, u32[]{:S(2)}) collective-permute-start(bf16[256,256]{1,0:T(8,128)(2,1)} %get-tuple-element.60), channel_id=1, source_target_pairs={{0,4},{1,5},{2,6},{3,7},{4,0},{5,1},{6,2},{7,3},{8,12},{9,13},{10,... | collective-permute-start | bytes 393224 | tf_op jit(solution)/shard_map/ppermute | solution.py:253
  97.9 6.0 %sum1.1 = (f32[256,256]{1,0:T(8,128)}, bf16[256,256]{1,0:T(8,128)(2,1)}, bf16[256,256]{1,0:T(8,128)(2,1)}, bf16[256,256]{1,0:T(8,128)(2,1)}) custom-call(s32[8,768]{1,0:T(8,128)} %get-tuple-element.43.refs_0_, bf16[768,256]{1,0:T(8,128)(2,1)} %get-tuple-element.46.refs_1_, bf16[768,256]{1,0:T(8,128)(2,1)} %copy-done.20, bf16[768,256]{1,0:T(8,128)(2,1)} %copy-done.21, ...), custom_call_target="tpu_custom_call" | custom-call | flops 3221225472 | bytes 3825664 | tf_op jit(solution)/shard_map/sum1/pallas_call | solution.py:222
  105.9 2.3 %collective-permute-start.8 = (bf16[272,256]{1,0:T(8,128)(2,1)S(1)}, bf16[272,256]{1,0:T(8,128)(2,1)S(1)}, u32[]{:S(2)}, u32[]{:S(2)}) collective-permute-start(bf16[272,256]{1,0:T(8,128)(2,1)S(1)} %copy-done.34), channel_id=1, source_target_pairs={{0,4},{1,5},{2,6},{3,7},{4,0},{5,1},{6,2},{7,3},{8,12},{9,13},{10,... | collective-permute-start | bytes 417800 | tf_op jit(solution)/shard_map/ppermute | solution.py:253
  109.7 2.0 %collective-permute-start.18 = (bf16[256,256]{1,0:T(8,128)(2,1)}, bf16[256,256]{1,0:T(8,128)(2,1)S(1)}, u32[]{:S(2)}, u32[]{:S(2)}) collective-permute-start(bf16[256,256]{1,0:T(8,128)(2,1)} %get-tuple-element.52), channel_id=1, source_target_pairs={{0,4},{1,5},{2,6},{3,7},{4,0},{5,1},{6,2},{7,3},{8,12},{9,13},{10,... | collective-permute-start | bytes 393224 | tf_op jit(solution)/shard_map/ppermute | solution.py:253
  111.7 1.7 %collective-permute-done.17.refs_7_ = bf16[256,256]{1,0:T(8,128)(2,1)S(1)} collective-permute-done((bf16[256,256]{1,0:T(8,128)(2,1)}, bf16[256,256]{1,0:T(8,128)(2,1)S(1)}, u32[]{:S(2)}, u32[]{:S(2)}) %collective-permute-start.17) | collective-permute-done | bytes 131104 | tf_op jit(solution)/shard_map/ppermute | solution.py:253
  113.4 2.6 %collective-permute-start.19 = (bf16[256,256]{1,0:T(8,128)(2,1)}, bf16[256,256]{1,0:T(8,128)(2,1)S(1)}, u32[]{:S(2)}, u32[]{:S(2)}) collective-permute-start(bf16[256,256]{1,0:T(8,128)(2,1)} %get-tuple-element.53), channel_id=1, source_target_pairs={{0,6},{1,7},{2,4},{3,5},{4,2},{5,3},{6,0},{7,1},{8,14},{9,15},{10,... | collective-permute-start | bytes 393224 | tf_op jit(solution)/shard_map/ppermute | solution.py:253
  116.0 14.3 %collective-permute-done.18.refs_8_ = bf16[256,256]{1,0:T(8,128)(2,1)S(1)} collective-permute-done((bf16[256,256]{1,0:T(8,128)(2,1)}, bf16[256,256]{1,0:T(8,128)(2,1)S(1)}, u32[]{:S(2)}, u32[]{:S(2)}) %collective-permute-start.18) | collective-permute-done | bytes 131104 | tf_op jit(solution)/shard_map/ppermute | solution.py:253
  131.2 2.7 %close.1 = (f32[256,768]{1,0:T(8,128)}, s32[1,256]{1,0:T(1,128)}, s32[1,256]{1,0:T(1,128)}) custom-call(s32[1,256]{1,0:T(1,128)} %bitcast.4, f32[8,256]{1,0:T(8,128)} %get-tuple-element.38.refs_1_, f32[256,256]{1,0:T(8,128)} %get-tuple-element.39.refs_2_, bf16[272,256]{1,0:T(8,128)(2,1)} %copy-done, bf16[272,256]{1,0:T(8,128)(2,1)} %copy-done.1, ...), custom_call_target="tpu_custom_call" | custom-call | flops 786432 | bytes 2788352 | tf_op jit(solution)/shard_map/close/pallas_call | solution.py:222
  (116 shorter events, 14.4 us)
Async XLA Ops:
  18.3 13.6 %collective-permute-start.20 = (bf16[768,256]{1,0:T(8,128)(2,1)}, bf16[768,256]{1,0:T(8,128)(2,1)S(1)}, u32[]{:S(2)}, u32[]{:S(2)}) collective-permute-start(bf16[768,256]{1,0:T(8,128)(2,1)} %get-tuple-element.55), channel_id=1, source_target_pairs={{0,8},{8,0},{16,24},{24,16},{1,9},{9,1},{17,25},{25,17},{2,10},{10... | collective-permute-start | bytes 1179656 | tf_op jit(solution)/shard_map/ppermute | solution.py:253
  21.2 19.8 %collective-permute-start.21 = (bf16[768,256]{1,0:T(8,128)(2,1)}, bf16[768,256]{1,0:T(8,128)(2,1)S(1)}, u32[]{:S(2)}, u32[]{:S(2)}) collective-permute-start(bf16[768,256]{1,0:T(8,128)(2,1)} %get-tuple-element.56), channel_id=1, source_target_pairs={{0,16},{8,24},{16,0},{24,8},{1,17},{9,25},{17,1},{25,9},{2,18},{10... | collective-permute-start | bytes 1179656 | tf_op jit(solution)/shard_map/ppermute | solution.py:253
  22.7 18.8 %collective-permute-start.22 = (bf16[768,256]{1,0:T(8,128)(2,1)}, bf16[768,256]{1,0:T(8,128)(2,1)S(1)}, u32[]{:S(2)}, u32[]{:S(2)}) collective-permute-start(bf16[768,256]{1,0:T(8,128)(2,1)} %get-tuple-element.57), channel_id=1, source_target_pairs={{0,24},{8,16},{16,8},{24,0},{1,25},{9,17},{17,9},{25,1},{2,26},{10... | collective-permute-start | bytes 1179656 | tf_op jit(solution)/shard_map/ppermute | solution.py:253
  22.7 22.1 %collective-permute-start.23 = (bf16[768,256]{1,0:T(8,128)(2,1)}, bf16[768,256]{1,0:T(8,128)(2,1)S(1)}, u32[]{:S(2)}, u32[]{:S(2)}) collective-permute-start(bf16[768,256]{1,0:T(8,128)(2,1)} %get-tuple-element.54.refs_1_), channel_id=1, source_target_pairs={{0,1},{1,0},{2,3},{3,2},{4,5},{5,4},{6,7},{7,6},{8,9},{9,8},{10,11... | collective-permute-start | bytes 1179656 | tf_op jit(solution)/shard_map/ppermute | solution.py:253
  29.9 18.4 %collective-permute-start.10 = (bf16[768,256]{1,0:T(8,128)(2,1)}, bf16[768,256]{1,0:T(8,128)(2,1)S(1)}, u32[]{:S(2)}, u32[]{:S(2)}) collective-permute-start(bf16[768,256]{1,0:T(8,128)(2,1)} %get-tuple-element.47), channel_id=1, source_target_pairs={{0,8},{8,0},{16,24},{24,16},{1,9},{9,1},{17,25},{25,17},{2,10},{10... | collective-permute-start | bytes 1179656 | tf_op jit(solution)/shard_map/ppermute | solution.py:253
  31.9 25.9 %collective-permute-start.11 = (bf16[768,256]{1,0:T(8,128)(2,1)}, bf16[768,256]{1,0:T(8,128)(2,1)S(1)}, u32[]{:S(2)}, u32[]{:S(2)}) collective-permute-start(bf16[768,256]{1,0:T(8,128)(2,1)} %get-tuple-element.48), channel_id=1, source_target_pairs={{0,16},{8,24},{16,0},{24,8},{1,17},{9,25},{17,1},{25,9},{2,18},{10... | collective-permute-start | bytes 1179656 | tf_op jit(solution)/shard_map/ppermute | solution.py:253
  41.0 17.3 %collective-permute-start.12 = (bf16[768,256]{1,0:T(8,128)(2,1)}, bf16[768,256]{1,0:T(8,128)(2,1)S(1)}, u32[]{:S(2)}, u32[]{:S(2)}) collective-permute-start(bf16[768,256]{1,0:T(8,128)(2,1)} %get-tuple-element.49), channel_id=1, source_target_pairs={{0,24},{8,16},{16,8},{24,0},{1,25},{9,17},{17,9},{25,1},{2,26},{10... | collective-permute-start | bytes 1179656 | tf_op jit(solution)/shard_map/ppermute | solution.py:253
  41.5 24.0 %collective-permute-start = (bf16[800,256]{1,0:T(8,128)(2,1)S(1)}, bf16[800,256]{1,0:T(8,128)(2,1)S(1)}, u32[]{:S(2)}, u32[]{:S(2)}) collective-permute-start(bf16[800,256]{1,0:T(8,128)(2,1)S(1)} %copy-done.15), channel_id=1, source_target_pairs={{0,8},{8,0},{16,24},{24,16},{1,9},{9,1},{17,25},{25,17},{2,10},{10... | collective-permute-start | bytes 1228808 | tf_op jit(solution)/shard_map/ppermute | solution.py:253
  44.9 29.9 %collective-permute-start.1 = (bf16[800,256]{1,0:T(8,128)(2,1)S(1)}, bf16[800,256]{1,0:T(8,128)(2,1)S(1)}, u32[]{:S(2)}, u32[]{:S(2)}) collective-permute-start(bf16[800,256]{1,0:T(8,128)(2,1)S(1)} %copy-done.13), channel_id=1, source_target_pairs={{0,16},{8,24},{16,0},{24,8},{1,17},{9,25},{17,1},{25,9},{2,18},{10... | collective-permute-start | bytes 1228808 | tf_op jit(solution)/shard_map/ppermute | solution.py:253
  48.3 26.5 %collective-permute-start.2 = (bf16[800,256]{1,0:T(8,128)(2,1)S(1)}, bf16[800,256]{1,0:T(8,128)(2,1)S(1)}, u32[]{:S(2)}, u32[]{:S(2)}) collective-permute-start(bf16[800,256]{1,0:T(8,128)(2,1)S(1)} %copy-done.10), channel_id=1, source_target_pairs={{0,24},{8,16},{16,8},{24,0},{1,25},{9,17},{17,9},{25,1},{2,26},{10... | collective-permute-start | bytes 1228808 | tf_op jit(solution)/shard_map/ppermute | solution.py:253
  57.8 17.5 %collective-permute-start.3 = (bf16[800,256]{1,0:T(8,128)(2,1)S(1)}, bf16[800,256]{1,0:T(8,128)(2,1)S(1)}, u32[]{:S(2)}, u32[]{:S(2)}) collective-permute-start(bf16[800,256]{1,0:T(8,128)(2,1)S(1)} %copy-done.9), channel_id=1, source_target_pairs={{0,1},{1,0},{2,3},{3,2},{4,5},{5,4},{6,7},{7,6},{8,9},{9,8},{10,11... | collective-permute-start | bytes 1228808 | tf_op jit(solution)/shard_map/ppermute | solution.py:253
  58.2 17.2 %collective-permute-start.24 = (bf16[768,256]{1,0:T(8,128)(2,1)S(1)}, bf16[768,256]{1,0:T(8,128)(2,1)S(1)}, u32[]{:S(2)}, u32[]{:S(2)}) collective-permute-start(bf16[768,256]{1,0:T(8,128)(2,1)S(1)} %collective-permute-done.20.refs_2_), channel_id=1, source_target_pairs={{0,1},{1,0},{2,3},{3,2},{4,5},{5,4},{6,7},{7,6},{8,9},{9,8},{10,11... | collective-permute-start | bytes 1179656 | tf_op jit(solution)/shard_map/ppermute | solution.py:253
  77.7 15.7 %collective-permute-start.13 = (bf16[768,256]{1,0:T(8,128)(2,1)}, bf16[768,256]{1,0:T(8,128)(2,1)S(1)}, u32[]{:S(2)}, u32[]{:S(2)}) collective-permute-start(bf16[768,256]{1,0:T(8,128)(2,1)} %get-tuple-element.46.refs_1_), channel_id=1, source_target_pairs={{0,1},{1,0},{2,3},{3,2},{4,5},{5,4},{6,7},{7,6},{8,9},{9,8},{10,11... | collective-permute-start | bytes 1179656 | tf_op jit(solution)/shard_map/ppermute | solution.py:253
  77.9 18.2 %collective-permute-start.14 = (bf16[768,256]{1,0:T(8,128)(2,1)S(1)}, bf16[768,256]{1,0:T(8,128)(2,1)S(1)}, u32[]{:S(2)}, u32[]{:S(2)}) collective-permute-start(bf16[768,256]{1,0:T(8,128)(2,1)S(1)} %collective-permute-done.10.refs_2_), channel_id=1, source_target_pairs={{0,1},{1,0},{2,3},{3,2},{4,5},{5,4},{6,7},{7,6},{8,9},{9,8},{10,11... | collective-permute-start | bytes 1179656 | tf_op jit(solution)/shard_map/ppermute | solution.py:253
  78.2 18.1 %collective-permute-start.15 = (bf16[768,256]{1,0:T(8,128)(2,1)S(1)}, bf16[768,256]{1,0:T(8,128)(2,1)S(1)}, u32[]{:S(2)}, u32[]{:S(2)}) collective-permute-start(bf16[768,256]{1,0:T(8,128)(2,1)S(1)} %collective-permute-done.11.refs_3_), channel_id=1, source_target_pairs={{0,1},{1,0},{2,3},{3,2},{4,5},{5,4},{6,7},{7,6},{8,9},{9,8},{10,11... | collective-permute-start | bytes 1179656 | tf_op jit(solution)/shard_map/ppermute | solution.py:253
  78.4 18.0 %collective-permute-start.16 = (bf16[768,256]{1,0:T(8,128)(2,1)S(1)}, bf16[768,256]{1,0:T(8,128)(2,1)S(1)}, u32[]{:S(2)}, u32[]{:S(2)}) collective-permute-start(bf16[768,256]{1,0:T(8,128)(2,1)S(1)} %collective-permute-done.12.refs_4_), channel_id=1, source_target_pairs={{0,1},{1,0},{2,3},{3,2},{4,5},{5,4},{6,7},{7,6},{8,9},{9,8},{10,11... | collective-permute-start | bytes 1179656 | tf_op jit(solution)/shard_map/ppermute | solution.py:253
  91.9 14.0 %collective-permute-start.27 = (bf16[256,256]{1,0:T(8,128)(2,1)}, bf16[256,256]{1,0:T(8,128)(2,1)S(1)}, u32[]{:S(2)}, u32[]{:S(2)}) collective-permute-start(bf16[256,256]{1,0:T(8,128)(2,1)} %get-tuple-element.59), channel_id=1, source_target_pairs={{0,2},{1,3},{2,0},{3,1},{4,6},{5,7},{6,4},{7,5},{8,10},{9,11},{10,... | collective-permute-start | bytes 393224 | tf_op jit(solution)/shard_map/ppermute | solution.py:253
  93.5 14.7 %collective-permute-start.28 = (bf16[256,256]{1,0:T(8,128)(2,1)}, bf16[256,256]{1,0:T(8,128)(2,1)S(1)}, u32[]{:S(2)}, u32[]{:S(2)}) collective-permute-start(bf16[256,256]{1,0:T(8,128)(2,1)} %get-tuple-element.60), channel_id=1, source_target_pairs={{0,4},{1,5},{2,6},{3,7},{4,0},{5,1},{6,2},{7,3},{8,12},{9,13},{10,... | collective-permute-start | bytes 393224 | tf_op jit(solution)/shard_map/ppermute | solution.py:253
  96.1 13.6 %collective-permute-start.29 = (bf16[256,256]{1,0:T(8,128)(2,1)}, bf16[256,256]{1,0:T(8,128)(2,1)S(1)}, u32[]{:S(2)}, u32[]{:S(2)}) collective-permute-start(bf16[256,256]{1,0:T(8,128)(2,1)} %get-tuple-element.61), channel_id=1, source_target_pairs={{0,6},{1,7},{2,4},{3,5},{4,2},{5,3},{6,0},{7,1},{8,14},{9,15},{10,... | collective-permute-start | bytes 393224 | tf_op jit(solution)/shard_map/ppermute | solution.py:253
  104.5 25.8 %collective-permute-start.7 = (bf16[272,256]{1,0:T(8,128)(2,1)S(1)}, bf16[272,256]{1,0:T(8,128)(2,1)S(1)}, u32[]{:S(2)}, u32[]{:S(2)}) collective-permute-start(bf16[272,256]{1,0:T(8,128)(2,1)S(1)} %copy-done.35), channel_id=1, source_target_pairs={{0,2},{1,3},{2,0},{3,1},{4,6},{5,7},{6,4},{7,5},{8,10},{9,11},{10,... | collective-permute-start | bytes 417800 | tf_op jit(solution)/shard_map/ppermute | solution.py:253
  105.9 24.5 %collective-permute-start.8 = (bf16[272,256]{1,0:T(8,128)(2,1)S(1)}, bf16[272,256]{1,0:T(8,128)(2,1)S(1)}, u32[]{:S(2)}, u32[]{:S(2)}) collective-permute-start(bf16[272,256]{1,0:T(8,128)(2,1)S(1)} %copy-done.34), channel_id=1, source_target_pairs={{0,4},{1,5},{2,6},{3,7},{4,0},{5,1},{6,2},{7,3},{8,12},{9,13},{10,... | collective-permute-start | bytes 417800 | tf_op jit(solution)/shard_map/ppermute | solution.py:253
  108.2 22.2 %collective-permute-start.9 = (bf16[272,256]{1,0:T(8,128)(2,1)S(1)}, bf16[272,256]{1,0:T(8,128)(2,1)S(1)}, u32[]{:S(2)}, u32[]{:S(2)}) collective-permute-start(bf16[272,256]{1,0:T(8,128)(2,1)S(1)} %copy-done.33), channel_id=1, source_target_pairs={{0,6},{1,7},{2,4},{3,5},{4,2},{5,3},{6,0},{7,1},{8,14},{9,15},{10,... | collective-permute-start | bytes 417800 | tf_op jit(solution)/shard_map/ppermute | solution.py:253
  109.7 20.6 %collective-permute-start.18 = (bf16[256,256]{1,0:T(8,128)(2,1)}, bf16[256,256]{1,0:T(8,128)(2,1)S(1)}, u32[]{:S(2)}, u32[]{:S(2)}) collective-permute-start(bf16[256,256]{1,0:T(8,128)(2,1)} %get-tuple-element.52), channel_id=1, source_target_pairs={{0,4},{1,5},{2,6},{3,7},{4,0},{5,1},{6,2},{7,3},{8,12},{9,13},{10,... | collective-permute-start | bytes 393224 | tf_op jit(solution)/shard_map/ppermute | solution.py:253
  113.4 16.9 %collective-permute-start.19 = (bf16[256,256]{1,0:T(8,128)(2,1)}, bf16[256,256]{1,0:T(8,128)(2,1)S(1)}, u32[]{:S(2)}, u32[]{:S(2)}) collective-permute-start(bf16[256,256]{1,0:T(8,128)(2,1)} %get-tuple-element.53), channel_id=1, source_target_pairs={{0,6},{1,7},{2,4},{3,5},{4,2},{5,3},{6,0},{7,1},{8,14},{9,15},{10,... | collective-permute-start | bytes 393224 | tf_op jit(solution)/shard_map/ppermute | solution.py:253
  (42 other events, 589.7 us)

commit v2 on v1

--- a/solution.py
+++ b/solution.py
@@ -6,6 +6,7 @@
 from jax.experimental import pallas as pl
 from jax.experimental.pallas import tpu as pltpu
 from jax.sharding import PartitionSpec as P
+
 
 CHUNKS = 3
 F32 = jnp.float32
@@ -50,6 +51,8 @@
     while step < vecs:
         run = run + jnp.where(lane >= step, pltpu.roll(run, step, 1), 0.0)
         step *= 2
+    over = jnp.max(hot(run > float(slots)), axis=1, keepdims=True)
+    over = jnp.max(over, axis=0, keepdims=True)
     rank = jnp.sum((run - member) * member, axis=0, keepdims=True).astype(jnp.int32)
     slot = jnp.where(rank < slots, group * slots + rank, -1)
     tags = jnp.where(
@@ -57,16 +60,15 @@
         (owner_col + 1).astype(F32),
         jnp.where(iota((16, vecs), 0) == 1, in_list.astype(F32), 0.0),
     )
-    return slot, tags.astype(BF16)
+    return slot, tags.astype(BF16), over
 
 
 def pack_kernel(first, slots, base, width, dsub, lists_here, row_count, col_count, *refs):
     if first:
-        ids_ref, codes_ref, res_ref, rot_ref, book_ref = refs[:5]
+        ids_ref, ct_ref, res_ref, rot_ref, book_ref = refs[:5]
         outs = refs[5 : 5 + row_count]
-        slot_ref, ct_ref, rot_t, tab_t, err_t = refs[5 + row_count :]
-        ct_ref[...] = codes_ref[...].T
-        slot, tags = plan_slots(ids_ref[...], slots, lists_here, row_count, col_count)
+        slot_ref, rot_t, tab_t, err_t = refs[5 + row_count :]
+        slot, tags, over = plan_slots(ids_ref[...], slots, lists_here, row_count, col_count)
         slot_ref[...] = jnp.broadcast_to(slot, slot_ref.shape)
     else:
         slot_ref, ct_ref, res_ref, rot_ref, book_ref = refs[:5]
@@ -112,6 +114,7 @@
         outs[group][0:slots, :] = rows.astype(BF16)
         if first:
             line = lax.dot_general(tags, picker, NT, preferred_element_type=F32)[0:8, :]
+            line = jnp.where(iota(line.shape, 0) == 2, over, line)
             extra = outs[group].shape[0] - slots
             parts = [line[:, at : min(at + width, slots)] for at in range(0, slots, width)]
             parts = [
@@ -135,9 +138,11 @@
         me = lax.axis_index("col")
         zone, core = me // 2, me % 2
         keys = []
+        over = jnp.zeros((1, 1), F32)
         for ref in got:
             extra = ref[slots:, :].astype(F32)
             pieces = -(-slots // width)
+            over = over + extra[2:3, 0:1]
             line = jnp.concatenate([extra[8 * p : 8 * p + 8, :] for p in range(pieces)], 1)
             line = line[:, 0:slots].astype(jnp.int32)
             owner_col = line[0:1, :] - 1
@@ -177,14 +182,14 @@
             eye = iota((lists_here, lists_here), 0) == iota((lists_here, lists_here), 1)
             line = jnp.sum(jnp.where(eye, count, 0.0), axis=0, keepdims=True)
             if zone_at == 0:
-                count_ref[...] = jnp.broadcast_to(line, count_ref.shape)
+                count_ref[...] = jnp.where(iota(count_ref.shape, 0) == 2, over, line)
             else:
                 number = line.astype(jnp.int32)
                 high = (number >> 8).astype(F32)
                 low = (number & 255).astype(F32)
                 shape = (16, lists_here)
                 extra = jnp.where(
-                    iota(shape, 0) == 0, high, jnp.where(iota(shape, 0) == 1, low, 0.0)
+                    iota(shape, 0) == 0, high, jnp.where(iota(shape, 0) == 1, low, over)
                 )
                 if width > lists_here:
                     extra = jnp.concatenate([extra, jnp.zeros((16, width - lists_here), F32)], 1)
@@ -213,11 +218,101 @@
         drift_ref[:, chunk * width : (chunk + 1) * width] = total / divisor
 
 
+def decode_rows(codes, codebook):
+    vec_rows, sub_count = codes.shape
+    cent_count, feat_width = codebook.shape
+    sub_width = feat_width // sub_count
+    code_table = codebook.reshape(cent_count, sub_count, sub_width)
+    block_rows = 256
+    code_blocks = codes.reshape(vec_rows // block_rows, block_rows, sub_count)
+
+    def one_block(code_block):
+        picker = (
+            code_block[:, :, None] == jnp.arange(cent_count, dtype=jnp.int32)[None, None, :]
+        ).astype(jnp.bfloat16)
+        picked = jnp.einsum("bmk,kmj->bmj", picker, code_table, preferred_element_type=jnp.float32)
+        return picked.reshape(block_rows, feat_width)
+
+    return lax.map(one_block, code_blocks).reshape(vec_rows, feat_width)
+
+
+def sum_by_list(rows_in, tags_in, list_total):
+    picker = (tags_in[:, None] == jnp.arange(list_total, dtype=jnp.int32)[None, :]).astype(
+        jnp.bfloat16
+    )
+    list_sums = lax.dot_general(
+        picker, rows_in, (((0,), (0,)), ((), ())), preferred_element_type=jnp.float32
+    )
+    counts = jnp.sum(picker, axis=0, dtype=jnp.float32)
+    return (list_sums, counts)
+
+
+def rank_in_block(owner_block, owner_total):
+    vec_rows = owner_block.shape[0]
+    picker = (owner_block[:, None] == jnp.arange(owner_total, dtype=jnp.int32)[None, :]).astype(
+        jnp.bfloat16
+    )
+    later = (
+        jnp.arange(vec_rows, dtype=jnp.int32)[:, None]
+        > jnp.arange(vec_rows, dtype=jnp.int32)[None, :]
+    )
+    before = jnp.dot(later.astype(jnp.bfloat16), picker, preferred_element_type=jnp.float32)
+    return jnp.sum(before * picker.astype(jnp.float32), axis=1).astype(jnp.int32)
+
+
+def spread_all(residuals, codes, list_ids, rotation, codebook, list_fill):
+    row_count = lax.axis_size("row")
+    col_count = lax.axis_size("col")
+    owner_total = row_count * col_count
+    vec_rows, feat_width = residuals.shape
+    lists_here = list_fill.shape[0]
+    slot_cap = 3 * vec_rows // owner_total
+    rotated = jnp.dot(residuals, rotation, preferred_element_type=jnp.float32)
+    rebuilt = decode_rows(codes, codebook)
+    encode_error = (rotated - rebuilt).astype(jnp.bfloat16)
+    owner_block = list_ids // lists_here
+    slot_index = owner_block * slot_cap + rank_in_block(owner_block, owner_total)
+    send_rows = (
+        jnp.zeros((owner_total * slot_cap, feat_width), jnp.bfloat16)
+        .at[slot_index]
+        .set(encode_error)
+    )
+    send_tags = jnp.full((owner_total * slot_cap,), -1, jnp.int32).at[slot_index].set(list_ids)
+    send_rows = send_rows.reshape(row_count, col_count, slot_cap, feat_width)
+    send_tags = send_tags.reshape(row_count, col_count, slot_cap)
+    got_rows, got_tags = (
+        lax.all_to_all(
+            lax.all_to_all(send_rows, "row", split_axis=0, concat_axis=0, tiled=True),
+            "col",
+            split_axis=1,
+            concat_axis=1,
+            tiled=True,
+        ),
+        lax.all_to_all(
+            lax.all_to_all(send_tags, "row", split_axis=0, concat_axis=0, tiled=True),
+            "col",
+            split_axis=1,
+            concat_axis=1,
+            tiled=True,
+        ),
+    )
+    got_rows = got_rows.reshape(-1, feat_width)
+    got_tags = got_tags.reshape(-1)
+    list_base = (lax.axis_index("row") * col_count + lax.axis_index("col")) * lists_here
+    local_index = jnp.where(got_tags >= 0, got_tags - list_base, -1)
+    list_sums, counts = sum_by_list(got_rows, local_index, lists_here)
+    list_counts = counts.astype(jnp.int32)
+    divisor = jnp.maximum(list_counts, 1).astype(jnp.float32)
+    list_drift = list_sums / divisor[:, None]
+    new_blocks = (list_fill + list_counts + 127) // 128 - (list_fill + 127) // 128
+    return (list_drift, list_counts, new_blocks)
+
+
 def vmem(count):
     return [pl.BlockSpec(memory_space=pltpu.VMEM)] * count
 
 
-def call(kernel, outs, scratch, ins, name, flops, specs=None):
+def call(kernel, outs, scratch, ins, flops, specs=None):
     size = sum(a.size * a.dtype.itemsize for a in (*ins, *outs))
     return pl.pallas_call(
         kernel,
@@ -226,7 +321,6 @@
         out_specs=vmem(len(outs)),
         scratch_shapes=scratch,
         grid=() if specs is None else (1,),
-        name=name,
         cost_estimate=pl.CostEstimate(flops=flops, bytes_accessed=size, transcendentals=0),
         compiler_params=pltpu.CompilerParams(vmem_limit_bytes=56 * 1024 * 1024),
     )(*ins)
@@ -247,7 +341,8 @@
     zone_count = col_count // 2
     width = split(feats, CHUNKS)
     chunks = feats // width
-    slots = 3 * vecs // row_count
+    bound = 3 * vecs // row_count
+    slots = up(bound // 2, 16)
 
     def trade(array, axis, size, mask):
         return lax.ppermute(array, axis, [(i, i ^ mask) for i in range(size)])
@@ -256,7 +351,7 @@
     fill = list_fill.reshape(1, lists_here)
     extra = tag_rows(slots, width)
     packed = []
-    slot = codes_t = None
+    slot = None
     for chunk in range(chunks):
         first = chunk == 0
         outs = [shape((slots + (extra if first else 0), width), BF16) for _ in range(row_count)]
@@ -266,11 +361,8 @@
             pltpu.VMEM((width, vecs), BF16),
         ]
         if first:
-            outs += [shape((8, vecs), jnp.int32), shape((subs, vecs), jnp.int32)]
-            lead = (ids, codes)
-        else:
-            lead = (slot, codes_t)
-        ins = (*lead, residuals, rotation, codebook)
+            outs += [shape((8, vecs), jnp.int32)]
+        ins = (ids if first else slot, codes.T, residuals, rotation, codebook)
 
         def all_of(array):
             return pl.BlockSpec(array.shape, lambda i: (0, 0))
@@ -286,13 +378,12 @@
             outs,
             scratch,
             ins,
-            f"pack{chunk}",
             2 * vecs * width * (feats + row_count * slots),
             specs,
         )
         packed.append(got[:row_count])
         if first:
-            slot, codes_t = got[row_count:]
+            slot = got[row_count]
     blocks = []
     key = count = None
     for chunk in range(chunks):
@@ -301,7 +392,8 @@
         got = [mine[0]] + [None] * (row_count - 1)
         for mask in sorted(range(1, row_count), key=lambda m: -bin(m).count("1")):
             got[mask] = trade(mine[mask], "row", row_count, mask)
-        other = [trade(array, "col", col_count, 1) for array in got]
+        other = [trade(got[0], "col", col_count, 1)]
+        other += [trade(array, "col", col_count, 1) for array in got[1:]]
         outs = [shape((lists_here, width), F32)]
         outs += [
             shape((lists_here + (16 if first else 0), width), BF16) for _ in range(zone_count - 1)
@@ -316,7 +408,6 @@
             outs,
             [pltpu.VMEM((2 * row_count * slots, width), BF16)],
             ins,
-            f"sum{chunk}",
             2 * zone_count * lists_here * 2 * row_count * slots * width,
         )
         if first:
@@ -330,19 +421,30 @@
         for mask in sorted(range(1, zone_count), key=lambda m: -m):
             got[mask] = trade(mine[mask], "col", col_count, 2 * mask)
         landed += got[1:]
-    drift, counts, new_blocks = call(
-        functools.partial(close_kernel, lists_here, width, chunks, zone_count),
-        [
-            shape((lists_here, feats), F32),
-            shape((1, lists_here), jnp.int32),
-            shape((1, lists_here), jnp.int32),
-        ],
-        [],
-        [fill, count, *landed],
-        "close",
-        lists_here * feats * zone_count,
-    )
-    return drift, counts.reshape(-1), new_blocks.reshape(-1)
+    over = count[2, 0]
+    for array in landed[1:zone_count]:
+        over = over + array[lists_here + 2, 0].astype(F32)
+
+    def close(*arrays):
+        drift, counts, new_blocks = call(
+            functools.partial(close_kernel, lists_here, width, chunks, zone_count),
+            [
+                shape((lists_here, feats), F32),
+                shape((1, lists_here), jnp.int32),
+                shape((1, lists_here), jnp.int32),
+            ],
+            [],
+            [fill, count, *arrays],
+            lists_here * feats * zone_count,
+        )
+        return drift, counts.reshape(-1), new_blocks.reshape(-1)
+
+    return lax.cond(
+        over > 0,
+        lambda *arrays: spread_all(residuals, codes, list_ids, rotation, codebook, list_fill),
+        close,
+        *landed,
+    )
 
 
 def solution(mesh):

time: 134 us -> 95.3 us (0.71)
  waiting for transfers between devices: 52.3 us -> 25.2 us
  Pallas kernels: 44 us -> 30.3 us
  between operations: 0.91 us -> 3.5 us
  local copies, waits for them, and re-layouts: 4.68 us -> 2.56 us
    ppermute x30, waiting for transfers between devices: 52.3 us -> 25.2 us  [trade(): return lax.ppermute(array, axis, [(i, i ^ mask) for i in range(size)])]
    pallas_call x7, Pallas kernels: 44 us -> 30.3 us  [call(): pl.pallas_call(kernel, out_shape=outs, in_specs=specs or vmem(len(ins)),...]
    unnamed x73 -> x68, local copies, waits for them, and re-layouts: 4.68 us -> 0.5 us
    slice x0 -> x4, local copies, waits for them, and re-layouts: none -> 2.06 us  [the longest x3 1.55 us: local(): over = over + array[lists_here + 2, 0].astype(F32)]
  transfers between devices with their start and end apart: 30 -> 30, of which waited for: 9 -> 9; matrix products, arithmetic and copies ran while one was open for 0% -> 2% of each run, Pallas kernels for 19% -> 18%
where the time goes in v2:
time: 95.3 us; the launch traced here: 94.6 us
  starting transfers between devices  33.1 us (35%)
  Pallas kernels  30.3 us (32%)
  waiting for transfers between devices  25.2 us (26%)
  between operations  3.5 us (4%)
  local copies, waits for them, and re-layouts  2.56 us (3%)
    ppermute x30, starting transfers between devices, trade(): return lax.ppermute(array, axis, [(i, i ^ mask) for i in range(size)])  33.1 us
    pallas_call x7, Pallas kernels, call(): pl.pallas_call(kernel, out_shape=outs, in_specs=specs or vmem(len(ins)),...  30.3 us
    ppermute x30, waiting for transfers between devices, trade(): return lax.ppermute(array, axis, [(i, i ^ mask) for i in range(size)])  25.2 us
  transfers between devices with their start and end apart: 30, of which 9 were waited for; matrix products, arithmetic and copies ran while one was open for 2% of the time, Pallas kernels for 18%

profile of v2, /device:TPU:0, one launch (start us, length us, event | category | flops | bytes accessed | tf_op | source)
XLA Modules:
  0.0 94.6 jit_solution(13640769471135770930)
XLA Ops:
  0.7 6.9 %shard_map.89 = (bf16[400,256]{1,0:T(8,128)(2,1)}, bf16[400,256]{1,0:T(8,128)(2,1)}, bf16[400,256]{1,0:T(8,128)(2,1)}, bf16[400,256]{1,0:T(8,128)(2,1)}, s32[8,1024]{1,0:T(8,128)}) custom-call(s32[1,1024]{1,0:T(1,128)} %bitcast.39, s32[64,1024]{1,0:T(8,128)} %bitcast.36, bf16[1024,768]{1,0:T(8,128)(2,1)} %refs_2_.5, bf16[768,768]{1,0:T(8,128)(2,1)} %refs_3_.5, ...), custom_call_target="tpu_custom_call" | custom-call | flops 1207959552 | bytes 4263936 | tf_op jit(solution)/shard_map/pallas_call | solution.py:317
  7.6 5.0 %shard_map.91 = (bf16[384,256]{1,0:T(8,128)(2,1)}, bf16[384,256]{1,0:T(8,128)(2,1)}, bf16[384,256]{1,0:T(8,128)(2,1)}, bf16[384,256]{1,0:T(8,128)(2,1)}) custom-call(s32[8,1024]{1,0:T(8,128)} %get-tuple-element.126.refs_0_, s32[64,1024]{1,0:T(8,128)S(1)} %bitcast.37, bf16[1024,768]{1,0:T(8,128)(2,1)S(1)} %copy-done.5, bf16[768,768]{1,0:T(8,128)(2,1)S(1)} %copy-done.6, ...), custom_call_target="tpu_custom_call" | custom-call | flops 1207959552 | bytes 4227072 | tf_op jit(solution)/shard_map/pallas_call | solution.py:317
  12.6 3.0 %collective-permute-start.10 = (bf16[384,256]{1,0:T(8,128)(2,1)}, bf16[384,256]{1,0:T(8,128)(2,1)S(1)}, u32[]{:S(2)}, u32[]{:S(2)}) collective-permute-start(bf16[384,256]{1,0:T(8,128)(2,1)} %get-tuple-element.128), channel_id=1, source_target_pairs={{0,8},{8,0},{16,24},{24,16},{1,9},{9,1},{17,25},{25,17},{2,10},{10... | collective-permute-start | bytes 589832 | tf_op jit(solution)/shard_map/ppermute | solution.py:348
  15.6 1.5 %collective-permute-start.11 = (bf16[384,256]{1,0:T(8,128)(2,1)}, bf16[384,256]{1,0:T(8,128)(2,1)S(1)}, u32[]{:S(2)}, u32[]{:S(2)}) collective-permute-start(bf16[384,256]{1,0:T(8,128)(2,1)} %get-tuple-element.129), channel_id=1, source_target_pairs={{0,16},{8,24},{16,0},{24,8},{1,17},{9,25},{17,1},{25,9},{2,18},{10... | collective-permute-start | bytes 589832 | tf_op jit(solution)/shard_map/ppermute | solution.py:348
  17.2 5.0 %shard_map.93 = (bf16[384,256]{1,0:T(8,128)(2,1)}, bf16[384,256]{1,0:T(8,128)(2,1)}, bf16[384,256]{1,0:T(8,128)(2,1)}, bf16[384,256]{1,0:T(8,128)(2,1)}) custom-call(s32[8,1024]{1,0:T(8,128)} %get-tuple-element.126.refs_0_, s32[64,1024]{1,0:T(8,128)S(1)} %bitcast.38, bf16[1024,768]{1,0:T(8,128)(2,1)S(1)} %copy-done.5, bf16[768,768]{1,0:T(8,128)(2,1)S(1)} %copy-done.6, ...), custom_call_target="tpu_custom_call" | custom-call | flops 1207959552 | bytes 4227072 | tf_op jit(solution)/shard_map/pallas_call | solution.py:317
  22.1 1.9 %collective-permute-start.20 = (bf16[384,256]{1,0:T(8,128)(2,1)}, bf16[384,256]{1,0:T(8,128)(2,1)S(1)}, u32[]{:S(2)}, u32[]{:S(2)}) collective-permute-start(bf16[384,256]{1,0:T(8,128)(2,1)} %get-tuple-element.136), channel_id=1, source_target_pairs={{0,8},{8,0},{16,24},{24,16},{1,9},{9,1},{17,25},{25,17},{2,10},{10... | collective-permute-start | bytes 589832 | tf_op jit(solution)/shard_map/ppermute | solution.py:348
  24.1 1.5 %collective-permute-start.21 = (bf16[384,256]{1,0:T(8,128)(2,1)}, bf16[384,256]{1,0:T(8,128)(2,1)S(1)}, u32[]{:S(2)}, u32[]{:S(2)}) collective-permute-start(bf16[384,256]{1,0:T(8,128)(2,1)} %get-tuple-element.137), channel_id=1, source_target_pairs={{0,16},{8,24},{16,0},{24,8},{1,17},{9,25},{17,1},{25,9},{2,18},{10... | collective-permute-start | bytes 589832 | tf_op jit(solution)/shard_map/ppermute | solution.py:348
  27.9 1.5 %collective-permute-start = (bf16[400,256]{1,0:T(8,128)(2,1)S(1)}, bf16[400,256]{1,0:T(8,128)(2,1)S(1)}, u32[]{:S(2)}, u32[]{:S(2)}) collective-permute-start(bf16[400,256]{1,0:T(8,128)(2,1)S(1)} %copy-done.13), channel_id=1, source_target_pairs={{0,8},{8,0},{16,24},{24,16},{1,9},{9,1},{17,25},{25,17},{2,10},{10... | collective-permute-start | bytes 614408 | tf_op jit(solution)/shard_map/ppermute | solution.py:348
  30.1 2.9 %collective-permute-start.2 = (bf16[400,256]{1,0:T(8,128)(2,1)S(1)}, bf16[400,256]{1,0:T(8,128)(2,1)S(1)}, u32[]{:S(2)}, u32[]{:S(2)}) collective-permute-start(bf16[400,256]{1,0:T(8,128)(2,1)S(1)} %copy-done.9), channel_id=1, source_target_pairs={{0,24},{8,16},{16,8},{24,0},{1,25},{9,17},{17,9},{25,1},{2,26},{10... | collective-permute-start | bytes 614408 | tf_op jit(solution)/shard_map/ppermute | solution.py:348
  33.0 3.3 %collective-permute-done.21.refs_3_ = bf16[384,256]{1,0:T(8,128)(2,1)S(1)} collective-permute-done((bf16[384,256]{1,0:T(8,128)(2,1)}, bf16[384,256]{1,0:T(8,128)(2,1)S(1)}, u32[]{:S(2)}, u32[]{:S(2)}) %collective-permute-start.21) | collective-permute-done | bytes 196640 | tf_op jit(solution)/shard_map/ppermute | solution.py:348
  36.8 2.9 %collective-permute-done.refs_1_ = bf16[400,256]{1,0:T(8,128)(2,1)S(1)} collective-permute-done((bf16[400,256]{1,0:T(8,128)(2,1)S(1)}, bf16[400,256]{1,0:T(8,128)(2,1)S(1)}, u32[]{:S(2)}, u32[]{:S(2)}) %collective-permute-start) | collective-permute-done | bytes 204832 | tf_op jit(solution)/shard_map/ppermute | solution.py:348
  39.8 4.6 %collective-permute-done.1.refs_2_ = bf16[400,256]{1,0:T(8,128)(2,1)S(1)} collective-permute-done((bf16[400,256]{1,0:T(8,128)(2,1)S(1)}, bf16[400,256]{1,0:T(8,128)(2,1)S(1)}, u32[]{:S(2)}, u32[]{:S(2)}) %collective-permute-start.1) | collective-permute-done | bytes 204832 | tf_op jit(solution)/shard_map/ppermute | solution.py:348
  47.8 4.4 %shard_map.90 = (f32[256,256]{1,0:T(8,128)S(1)}, bf16[272,256]{1,0:T(8,128)(2,1)}, bf16[272,256]{1,0:T(8,128)(2,1)}, bf16[272,256]{1,0:T(8,128)(2,1)}, f32[8,256]{1,0:T(8,128)S(1)}, /*index=5*/s32[8,384]{1,0:T(8,128)}) custom-call(bf16[400,256]{1,0:T(8,128)(2,1)} %get-tuple-element.116.refs_0_, bf16[400,256]{1,0:T(8,128)(2,1)} %copy-done.8, ...), custom_call_target="tpu_custom_call" | custom-call | flops 1610612736 | bytes 2338816 | tf_op jit(solution)/shard_map/pallas_call | solution.py:317
  52.2 1.6 %collective-permute-start.7 = (bf16[272,256]{1,0:T(8,128)(2,1)}, bf16[272,256]{1,0:T(8,128)(2,1)S(1)}, u32[]{:S(2)}, u32[]{:S(2)}) collective-permute-start(bf16[272,256]{1,0:T(8,128)(2,1)} %get-tuple-element.121), channel_id=1, source_target_pairs={{0,2},{1,3},{2,0},{3,1},{4,6},{5,7},{6,4},{7,5},{8,10},{9,11},{10,... | collective-permute-start | bytes 417800 | tf_op jit(solution)/shard_map/ppermute | solution.py:348
  53.9 4.0 %shard_map.92 = (f32[256,256]{1,0:T(8,128)S(1)}, bf16[256,256]{1,0:T(8,128)(2,1)}, bf16[256,256]{1,0:T(8,128)(2,1)}, bf16[256,256]{1,0:T(8,128)(2,1)}) custom-call(s32[8,384]{1,0:T(8,128)} %get-tuple-element.125.refs_0_, bf16[384,256]{1,0:T(8,128)(2,1)} %get-tuple-element.127.refs_1_, bf16[384,256]{1,0:T(8,128)(2,1)} %copy-done.21, ...), custom_call_target="tpu_custom_call" | custom-call | flops 1610612736 | bytes 2240512 | tf_op jit(solution)/shard_map/pallas_call | solution.py:317
  57.9 2.7 %collective-permute-start.8 = (bf16[272,256]{1,0:T(8,128)(2,1)S(1)}, bf16[272,256]{1,0:T(8,128)(2,1)S(1)}, u32[]{:S(2)}, u32[]{:S(2)}) collective-permute-start(bf16[272,256]{1,0:T(8,128)(2,1)S(1)} %copy-done.33), channel_id=1, source_target_pairs={{0,4},{1,5},{2,6},{3,7},{4,0},{5,1},{6,2},{7,3},{8,12},{9,13},{10,... | collective-permute-start | bytes 417800 | tf_op jit(solution)/shard_map/ppermute | solution.py:348
  61.5 3.5 %collective-permute-start.18 = (bf16[256,256]{1,0:T(8,128)(2,1)}, bf16[256,256]{1,0:T(8,128)(2,1)S(1)}, u32[]{:S(2)}, u32[]{:S(2)}) collective-permute-start(bf16[256,256]{1,0:T(8,128)(2,1)} %get-tuple-element.133), channel_id=1, source_target_pairs={{0,4},{1,5},{2,6},{3,7},{4,0},{5,1},{6,2},{7,3},{8,12},{9,13},{10,... | collective-permute-start | bytes 393224 | tf_op jit(solution)/shard_map/ppermute | solution.py:348
  65.1 4.0 %shard_map.94 = (f32[256,256]{1,0:T(8,128)S(1)}, bf16[256,256]{1,0:T(8,128)(2,1)}, bf16[256,256]{1,0:T(8,128)(2,1)}, bf16[256,256]{1,0:T(8,128)(2,1)}) custom-call(s32[8,384]{1,0:T(8,128)} %get-tuple-element.125.refs_0_, bf16[384,256]{1,0:T(8,128)(2,1)} %get-tuple-element.135.refs_1_, bf16[384,256]{1,0:T(8,128)(2,1)} %copy-done.18, ...), custom_call_target="tpu_custom_call" | custom-call | flops 1610612736 | bytes 2240512 | tf_op jit(solution)/shard_map/pallas_call | solution.py:317
  69.1 2.7 %collective-permute-done.17 = bf16[256,256]{1,0:T(8,128)(2,1)S(1)} collective-permute-done((bf16[256,256]{1,0:T(8,128)(2,1)}, bf16[256,256]{1,0:T(8,128)(2,1)S(1)}, u32[]{:S(2)}, u32[]{:S(2)}) %collective-permute-start.17) | collective-permute-done | bytes 131104 | tf_op jit(solution)/shard_map/ppermute | solution.py:348
  71.7 2.9 %collective-permute-start.19 = (bf16[256,256]{1,0:T(8,128)(2,1)S(1)}, bf16[256,256]{1,0:T(8,128)(2,1)S(1)}, u32[]{:S(2)}, u32[]{:S(2)}) collective-permute-start(bf16[256,256]{1,0:T(8,128)(2,1)S(1)} %copy-done.34), channel_id=1, source_target_pairs={{0,6},{1,7},{2,4},{3,5},{4,2},{5,3},{6,0},{7,1},{8,14},{9,15},{10,... | collective-permute-start | bytes 393224 | tf_op jit(solution)/shard_map/ppermute | solution.py:348
  74.6 1.5 %collective-permute-start.28 = (bf16[256,256]{1,0:T(8,128)(2,1)}, bf16[256,256]{1,0:T(8,128)(2,1)S(1)}, u32[]{:S(2)}, u32[]{:S(2)}) collective-permute-start(bf16[256,256]{1,0:T(8,128)(2,1)} %get-tuple-element.141), channel_id=1, source_target_pairs={{0,4},{1,5},{2,6},{3,7},{4,0},{5,1},{6,2},{7,3},{8,12},{9,13},{10,... | collective-permute-start | bytes 393224 | tf_op jit(solution)/shard_map/ppermute | solution.py:348
  76.1 2.9 %collective-permute-start.29 = (bf16[256,256]{1,0:T(8,128)(2,1)}, bf16[256,256]{1,0:T(8,128)(2,1)S(1)}, u32[]{:S(2)}, u32[]{:S(2)}) collective-permute-start(bf16[256,256]{1,0:T(8,128)(2,1)} %get-tuple-element.142), channel_id=1, source_target_pairs={{0,6},{1,7},{2,4},{3,5},{4,2},{5,3},{6,0},{7,1},{8,14},{9,15},{10,... | collective-permute-start | bytes 393224 | tf_op jit(solution)/shard_map/ppermute | solution.py:348
  83.7 4.2 %collective-permute-done.18 = bf16[256,256]{1,0:T(8,128)(2,1)S(1)} collective-permute-done((bf16[256,256]{1,0:T(8,128)(2,1)}, bf16[256,256]{1,0:T(8,128)(2,1)S(1)}, u32[]{:S(2)}, u32[]{:S(2)}) %collective-permute-start.18) | collective-permute-done | bytes 131104 | tf_op jit(solution)/shard_map/ppermute | solution.py:348
  87.9 5.6 %collective-permute-done.28 = bf16[256,256]{1,0:T(8,128)(2,1)S(1)} collective-permute-done((bf16[256,256]{1,0:T(8,128)(2,1)}, bf16[256,256]{1,0:T(8,128)(2,1)S(1)}, u32[]{:S(2)}, u32[]{:S(2)}) %collective-permute-start.28) | collective-permute-done | bytes 131104 | tf_op jit(solution)/shard_map/ppermute | solution.py:348
  (116 shorter events, 12.3 us)
Async XLA Ops:
  12.6 11.5 %collective-permute-start.10 = (bf16[384,256]{1,0:T(8,128)(2,1)}, bf16[384,256]{1,0:T(8,128)(2,1)S(1)}, u32[]{:S(2)}, u32[]{:S(2)}) collective-permute-start(bf16[384,256]{1,0:T(8,128)(2,1)} %get-tuple-element.128), channel_id=1, source_target_pairs={{0,8},{8,0},{16,24},{24,16},{1,9},{9,1},{17,25},{25,17},{2,10},{10... | collective-permute-start | bytes 589832 | tf_op jit(solution)/shard_map/ppermute | solution.py:348
  15.6 10.8 %collective-permute-start.11 = (bf16[384,256]{1,0:T(8,128)(2,1)}, bf16[384,256]{1,0:T(8,128)(2,1)S(1)}, u32[]{:S(2)}, u32[]{:S(2)}) collective-permute-start(bf16[384,256]{1,0:T(8,128)(2,1)} %get-tuple-element.129), channel_id=1, source_target_pairs={{0,16},{8,24},{16,0},{24,8},{1,17},{9,25},{17,1},{25,9},{2,18},{10... | collective-permute-start | bytes 589832 | tf_op jit(solution)/shard_map/ppermute | solution.py:348
  17.1 10.8 %collective-permute-start.12 = (bf16[384,256]{1,0:T(8,128)(2,1)}, bf16[384,256]{1,0:T(8,128)(2,1)S(1)}, u32[]{:S(2)}, u32[]{:S(2)}) collective-permute-start(bf16[384,256]{1,0:T(8,128)(2,1)} %get-tuple-element.130), channel_id=1, source_target_pairs={{0,24},{8,16},{16,8},{24,0},{1,25},{9,17},{17,9},{25,1},{2,26},{10... | collective-permute-start | bytes 589832 | tf_op jit(solution)/shard_map/ppermute | solution.py:348
  17.2 12.3 %collective-permute-start.13 = (bf16[384,256]{1,0:T(8,128)(2,1)}, bf16[384,256]{1,0:T(8,128)(2,1)S(1)}, u32[]{:S(2)}, u32[]{:S(2)}) collective-permute-start(bf16[384,256]{1,0:T(8,128)(2,1)} %get-tuple-element.127.refs_1_), channel_id=1, source_target_pairs={{0,1},{1,0},{2,3},{3,2},{4,5},{5,4},{6,7},{7,6},{8,9},{9,8},{10,11... | collective-permute-start | bytes 589832 | tf_op jit(solution)/shard_map/ppermute | solution.py:348
  24.1 12.2 %collective-permute-start.21 = (bf16[384,256]{1,0:T(8,128)(2,1)}, bf16[384,256]{1,0:T(8,128)(2,1)S(1)}, u32[]{:S(2)}, u32[]{:S(2)}) collective-permute-start(bf16[384,256]{1,0:T(8,128)(2,1)} %get-tuple-element.137), channel_id=1, source_target_pairs={{0,16},{8,24},{16,0},{24,8},{1,17},{9,25},{17,1},{25,9},{2,18},{10... | collective-permute-start | bytes 589832 | tf_op jit(solution)/shard_map/ppermute | solution.py:348
  26.4 9.9 %collective-permute-start.22 = (bf16[384,256]{1,0:T(8,128)(2,1)}, bf16[384,256]{1,0:T(8,128)(2,1)S(1)}, u32[]{:S(2)}, u32[]{:S(2)}) collective-permute-start(bf16[384,256]{1,0:T(8,128)(2,1)} %get-tuple-element.138), channel_id=1, source_target_pairs={{0,24},{8,16},{16,8},{24,0},{1,25},{9,17},{17,9},{25,1},{2,26},{10... | collective-permute-start | bytes 589832 | tf_op jit(solution)/shard_map/ppermute | solution.py:348
  27.9 11.8 %collective-permute-start = (bf16[400,256]{1,0:T(8,128)(2,1)S(1)}, bf16[400,256]{1,0:T(8,128)(2,1)S(1)}, u32[]{:S(2)}, u32[]{:S(2)}) collective-permute-start(bf16[400,256]{1,0:T(8,128)(2,1)S(1)} %copy-done.13), channel_id=1, source_target_pairs={{0,8},{8,0},{16,24},{24,16},{1,9},{9,1},{17,25},{25,17},{2,10},{10... | collective-permute-start | bytes 614408 | tf_op jit(solution)/shard_map/ppermute | solution.py:348
  29.5 14.9 %collective-permute-start.1 = (bf16[400,256]{1,0:T(8,128)(2,1)S(1)}, bf16[400,256]{1,0:T(8,128)(2,1)S(1)}, u32[]{:S(2)}, u32[]{:S(2)}) collective-permute-start(bf16[400,256]{1,0:T(8,128)(2,1)S(1)} %copy-done.11), channel_id=1, source_target_pairs={{0,16},{8,24},{16,0},{24,8},{1,17},{9,25},{17,1},{25,9},{2,18},{10... | collective-permute-start | bytes 614408 | tf_op jit(solution)/shard_map/ppermute | solution.py:348
  30.1 14.2 %collective-permute-start.2 = (bf16[400,256]{1,0:T(8,128)(2,1)S(1)}, bf16[400,256]{1,0:T(8,128)(2,1)S(1)}, u32[]{:S(2)}, u32[]{:S(2)}) collective-permute-start(bf16[400,256]{1,0:T(8,128)(2,1)S(1)} %copy-done.9), channel_id=1, source_target_pairs={{0,24},{8,16},{16,8},{24,0},{1,25},{9,17},{17,9},{25,1},{2,26},{10... | collective-permute-start | bytes 614408 | tf_op jit(solution)/shard_map/ppermute | solution.py:348
  36.3 8.6 %collective-permute-start.3 = (bf16[400,256]{1,0:T(8,128)(2,1)S(1)}, bf16[400,256]{1,0:T(8,128)(2,1)S(1)}, u32[]{:S(2)}, u32[]{:S(2)}) collective-permute-start(bf16[400,256]{1,0:T(8,128)(2,1)S(1)} %copy-done.7), channel_id=1, source_target_pairs={{0,1},{1,0},{2,3},{3,2},{4,5},{5,4},{6,7},{7,6},{8,9},{9,8},{10,11... | collective-permute-start | bytes 614408 | tf_op jit(solution)/shard_map/ppermute | solution.py:348
  36.3 8.6 %collective-permute-start.14 = (bf16[384,256]{1,0:T(8,128)(2,1)S(1)}, bf16[384,256]{1,0:T(8,128)(2,1)S(1)}, u32[]{:S(2)}, u32[]{:S(2)}) collective-permute-start(bf16[384,256]{1,0:T(8,128)(2,1)S(1)} %collective-permute-done.10.refs_2_), channel_id=1, source_target_pairs={{0,1},{1,0},{2,3},{3,2},{4,5},{5,4},{6,7},{7,6},{8,9},{9,8},{10,11... | collective-permute-start | bytes 589832 | tf_op jit(solution)/shard_map/ppermute | solution.py:348
  46.4 11.5 %collective-permute-start.23 = (bf16[384,256]{1,0:T(8,128)(2,1)}, bf16[384,256]{1,0:T(8,128)(2,1)S(1)}, u32[]{:S(2)}, u32[]{:S(2)}) collective-permute-start(bf16[384,256]{1,0:T(8,128)(2,1)} %get-tuple-element.135.refs_1_), channel_id=1, source_target_pairs={{0,1},{1,0},{2,3},{3,2},{4,5},{5,4},{6,7},{7,6},{8,9},{9,8},{10,11... | collective-permute-start | bytes 589832 | tf_op jit(solution)/shard_map/ppermute | solution.py:348
  46.6 14.0 %collective-permute-start.24 = (bf16[384,256]{1,0:T(8,128)(2,1)S(1)}, bf16[384,256]{1,0:T(8,128)(2,1)S(1)}, u32[]{:S(2)}, u32[]{:S(2)}) collective-permute-start(bf16[384,256]{1,0:T(8,128)(2,1)S(1)} %collective-permute-done.20.refs_2_), channel_id=1, source_target_pairs={{0,1},{1,0},{2,3},{3,2},{4,5},{5,4},{6,7},{7,6},{8,9},{9,8},{10,11... | collective-permute-start | bytes 589832 | tf_op jit(solution)/shard_map/ppermute | solution.py:348
  46.9 14.1 %collective-permute-start.25 = (bf16[384,256]{1,0:T(8,128)(2,1)S(1)}, bf16[384,256]{1,0:T(8,128)(2,1)S(1)}, u32[]{:S(2)}, u32[]{:S(2)}) collective-permute-start(bf16[384,256]{1,0:T(8,128)(2,1)S(1)} %collective-permute-done.21.refs_3_), channel_id=1, source_target_pairs={{0,1},{1,0},{2,3},{3,2},{4,5},{5,4},{6,7},{7,6},{8,9},{9,8},{10,11... | collective-permute-start | bytes 589832 | tf_op jit(solution)/shard_map/ppermute | solution.py:348
  47.1 14.4 %collective-permute-start.26 = (bf16[384,256]{1,0:T(8,128)(2,1)S(1)}, bf16[384,256]{1,0:T(8,128)(2,1)S(1)}, u32[]{:S(2)}, u32[]{:S(2)}) collective-permute-start(bf16[384,256]{1,0:T(8,128)(2,1)S(1)} %collective-permute-done.22.refs_4_), channel_id=1, source_target_pairs={{0,1},{1,0},{2,3},{3,2},{4,5},{5,4},{6,7},{7,6},{8,9},{9,8},{10,11... | collective-permute-start | bytes 589832 | tf_op jit(solution)/shard_map/ppermute | solution.py:348
  52.2 22.4 %collective-permute-start.7 = (bf16[272,256]{1,0:T(8,128)(2,1)}, bf16[272,256]{1,0:T(8,128)(2,1)S(1)}, u32[]{:S(2)}, u32[]{:S(2)}) collective-permute-start(bf16[272,256]{1,0:T(8,128)(2,1)} %get-tuple-element.121), channel_id=1, source_target_pairs={{0,2},{1,3},{2,0},{3,1},{4,6},{5,7},{6,4},{7,5},{8,10},{9,11},{10,... | collective-permute-start | bytes 417800 | tf_op jit(solution)/shard_map/ppermute | solution.py:348
  57.9 16.7 %collective-permute-start.8 = (bf16[272,256]{1,0:T(8,128)(2,1)S(1)}, bf16[272,256]{1,0:T(8,128)(2,1)S(1)}, u32[]{:S(2)}, u32[]{:S(2)}) collective-permute-start(bf16[272,256]{1,0:T(8,128)(2,1)S(1)} %copy-done.33), channel_id=1, source_target_pairs={{0,4},{1,5},{2,6},{3,7},{4,0},{5,1},{6,2},{7,3},{8,12},{9,13},{10,... | collective-permute-start | bytes 417800 | tf_op jit(solution)/shard_map/ppermute | solution.py:348
  60.6 15.6 %collective-permute-start.9 = (bf16[272,256]{1,0:T(8,128)(2,1)S(1)}, bf16[272,256]{1,0:T(8,128)(2,1)S(1)}, u32[]{:S(2)}, u32[]{:S(2)}) collective-permute-start(bf16[272,256]{1,0:T(8,128)(2,1)S(1)} %copy-done.32), channel_id=1, source_target_pairs={{0,6},{1,7},{2,4},{3,5},{4,2},{5,3},{6,0},{7,1},{8,14},{9,15},{10,... | collective-permute-start | bytes 417800 | tf_op jit(solution)/shard_map/ppermute | solution.py:348
  61.0 10.8 %collective-permute-start.17 = (bf16[256,256]{1,0:T(8,128)(2,1)}, bf16[256,256]{1,0:T(8,128)(2,1)S(1)}, u32[]{:S(2)}, u32[]{:S(2)}) collective-permute-start(bf16[256,256]{1,0:T(8,128)(2,1)} %get-tuple-element.132), channel_id=1, source_target_pairs={{0,2},{1,3},{2,0},{3,1},{4,6},{5,7},{6,4},{7,5},{8,10},{9,11},{10,... | collective-permute-start | bytes 393224 | tf_op jit(solution)/shard_map/ppermute | solution.py:348
  61.5 26.3 %collective-permute-start.18 = (bf16[256,256]{1,0:T(8,128)(2,1)}, bf16[256,256]{1,0:T(8,128)(2,1)S(1)}, u32[]{:S(2)}, u32[]{:S(2)}) collective-permute-start(bf16[256,256]{1,0:T(8,128)(2,1)} %get-tuple-element.133), channel_id=1, source_target_pairs={{0,4},{1,5},{2,6},{3,7},{4,0},{5,1},{6,2},{7,3},{8,12},{9,13},{10,... | collective-permute-start | bytes 393224 | tf_op jit(solution)/shard_map/ppermute | solution.py:348
  71.7 16.1 %collective-permute-start.19 = (bf16[256,256]{1,0:T(8,128)(2,1)S(1)}, bf16[256,256]{1,0:T(8,128)(2,1)S(1)}, u32[]{:S(2)}, u32[]{:S(2)}) collective-permute-start(bf16[256,256]{1,0:T(8,128)(2,1)S(1)} %copy-done.34), channel_id=1, source_target_pairs={{0,6},{1,7},{2,4},{3,5},{4,2},{5,3},{6,0},{7,1},{8,14},{9,15},{10,... | collective-permute-start | bytes 393224 | tf_op jit(solution)/shard_map/ppermute | solution.py:348
  74.6 13.2 %collective-permute-start.27 = (bf16[256,256]{1,0:T(8,128)(2,1)}, bf16[256,256]{1,0:T(8,128)(2,1)S(1)}, u32[]{:S(2)}, u32[]{:S(2)}) collective-permute-start(bf16[256,256]{1,0:T(8,128)(2,1)} %get-tuple-element.140), channel_id=1, source_target_pairs={{0,2},{1,3},{2,0},{3,1},{4,6},{5,7},{6,4},{7,5},{8,10},{9,11},{10,... | collective-permute-start | bytes 393224 | tf_op jit(solution)/shard_map/ppermute | solution.py:348
  74.6 18.8 %collective-permute-start.28 = (bf16[256,256]{1,0:T(8,128)(2,1)}, bf16[256,256]{1,0:T(8,128)(2,1)S(1)}, u32[]{:S(2)}, u32[]{:S(2)}) collective-permute-start(bf16[256,256]{1,0:T(8,128)(2,1)} %get-tuple-element.141), channel_id=1, source_target_pairs={{0,4},{1,5},{2,6},{3,7},{4,0},{5,1},{6,2},{7,3},{8,12},{9,13},{10,... | collective-permute-start | bytes 393224 | tf_op jit(solution)/shard_map/ppermute | solution.py:348
  76.1 17.3 %collective-permute-start.29 = (bf16[256,256]{1,0:T(8,128)(2,1)}, bf16[256,256]{1,0:T(8,128)(2,1)S(1)}, u32[]{:S(2)}, u32[]{:S(2)}) collective-permute-start(bf16[256,256]{1,0:T(8,128)(2,1)} %get-tuple-element.142), channel_id=1, source_target_pairs={{0,6},{1,7},{2,4},{3,5},{4,2},{5,3},{6,0},{7,1},{8,14},{9,15},{10,... | collective-permute-start | bytes 393224 | tf_op jit(solution)/shard_map/ppermute | solution.py:348
  (40 other events, 485.1 us)

commit v3 on v2

--- a/solution.py
+++ b/solution.py
@@ -8,7 +8,7 @@
 from jax.sharding import PartitionSpec as P
 
 
-CHUNKS = 3
+CUT = (2, 2, 2)
 F32 = jnp.float32
 BF16 = jnp.bfloat16
 NT = (((1,), (1,)), ((), ()))
@@ -28,12 +28,6 @@
 
 def hot(test):
     return jnp.where(test, 1.0, 0.0).astype(F32)
-
-
-def split(total, pieces):
-    while total % (128 * pieces):
-        pieces -= 1
-    return total // pieces
 
 
 def plan_slots(ids, slots, lists_here, row_count, col_count):
@@ -77,13 +71,14 @@
         slot = slot_ref[0:1, :]
     vecs = res_ref.shape[0]
     cents = book_ref.shape[0]
-    tab_t[...] = book_ref[...].astype(F32).T
+    here = slice(base, base + width)
+    tab_t[...] = book_ref[:, here].astype(F32).T
     rot_t[...] = lax.dot_general(
-        rot_ref[...], res_ref[...], (((0,), (1,)), ((), ())), preferred_element_type=F32
-    )
-
-    def lanes(block, carry):
-        here = pl.ds(pl.multiple_of(block * 128, 128), 128)
+        rot_ref[:, here], res_ref[...], (((0,), (1,)), ((), ())), preferred_element_type=F32
+    )
+
+    for block in range(vecs // 128):
+        here = slice(block * 128, (block + 1) * 128)
 
         def half(row):
             first_sub = (base + row) // dsub
@@ -104,37 +99,41 @@
 
         for row in range(0, width, 16):
             err_t[row : row + 16, here] = jnp.concatenate([half(row), half(row + 8)], 0).astype(BF16)
-        return carry
-
-    lax.fori_loop(0, vecs // 128, lanes, 0)
-    err = err_t[...]
+
+    picker = hot(iota((row_count * slots, vecs), 0) == slot).astype(BF16)
+    rows = lax.dot_general(picker, err_t[...], NT, preferred_element_type=F32).astype(BF16)
     for group in range(row_count):
-        picker = hot(iota((slots, vecs), 0) + group * slots == slot).astype(BF16)
-        rows = lax.dot_general(picker, err, NT, preferred_element_type=F32)
-        outs[group][0:slots, :] = rows.astype(BF16)
-        if first:
-            line = lax.dot_general(tags, picker, NT, preferred_element_type=F32)[0:8, :]
-            line = jnp.where(iota(line.shape, 0) == 2, over, line)
-            extra = outs[group].shape[0] - slots
-            parts = [line[:, at : min(at + width, slots)] for at in range(0, slots, width)]
-            parts = [
-                part
-                if part.shape[1] == width
-                else jnp.concatenate([part, jnp.zeros((8, width - part.shape[1]), F32)], 1)
-                for part in parts
-            ]
-            while len(parts) * 8 < extra:
-                parts.append(jnp.zeros((8, width), F32))
-            outs[group][slots:, :] = jnp.concatenate(parts, 0).astype(BF16)
+        outs[group][0:slots, :] = rows[group * slots : (group + 1) * slots, :]
+    if not first:
+        return
+    lines = lax.dot_general(tags, picker, NT, preferred_element_type=F32)[0:8, :]
+    lines = jnp.where(iota(lines.shape, 0) == 2, over, lines)
+    for group in range(row_count):
+        line = lines[:, group * slots : (group + 1) * slots]
+        extra = outs[group].shape[0] - slots
+        parts = [line[:, at : min(at + width, slots)] for at in range(0, slots, width)]
+        parts = [
+            part
+            if part.shape[1] == width
+            else jnp.concatenate([part, jnp.zeros((8, width - part.shape[1]), F32)], 1)
+            for part in parts
+        ]
+        while len(parts) * 8 < extra:
+            parts.append(jnp.zeros((8, width), F32))
+        outs[group][slots:, :] = jnp.concatenate(parts, 0).astype(BF16)
 
 
 def sum_kernel(first, slots, width, lists_here, row_count, zone_count, *refs):
     senders = 2 * row_count
-    lane_count = senders * slots
+    refs = list(refs)
+    key_in = None if first else refs.pop(0)
+    got, refs = refs[:senders], refs[senders:]
+    own, send = refs[:2]
+    rows = refs.pop()
+    kept = refs[2:3] if zone_count > 2 else []
+    over = None
     if first:
-        got = refs[:senders]
-        blocks = refs[senders : senders + zone_count]
-        count_ref, key_ref, rows = refs[senders + zone_count :]
+        count_ref, key_ref = refs[-2:]
         me = lax.axis_index("col")
         zone, core = me // 2, me % 2
         keys = []
@@ -152,21 +151,18 @@
         for b in range(senders):
             key_ref[b : b + 1, :] = keys[b]
     else:
-        key_ref = refs[0]
-        got = refs[1 : 1 + senders]
-        blocks = refs[1 + senders : 1 + senders + zone_count]
-        rows = refs[1 + senders + zone_count]
-        keys = [key_ref[b : b + 1, :] for b in range(senders)]
+        keys = [key_in[b : b + 1, :] for b in range(senders)]
     for b in range(senders):
         rows[b * slots : (b + 1) * slots, :] = got[b][0:slots, :]
     whole = slots % 128 == 0
     if whole:
         keys = [jnp.concatenate(keys, 1)]
-    span = lane_count if whole else slots
-    for zone_at in range(zone_count):
+    span = senders * slots if whole else slots
+    counts = []
+    for at in range(zone_count):
         total = count = None
         for b, key in enumerate(keys):
-            picker = hot(iota((lists_here, span), 0) + zone_at * lists_here == key)
+            picker = hot(iota((lists_here, span), 0) + at * lists_here == key)
             part = jnp.dot(
                 picker.astype(BF16), rows[b * span : (b + 1) * span, :], preferred_element_type=F32
             )
@@ -174,48 +170,101 @@
             if first:
                 part = jnp.sum(picker, axis=1, keepdims=True)
                 count = part if count is None else count + part
-        if zone_at == 0:
-            blocks[0][...] = total
-        else:
-            blocks[zone_at][0:lists_here, :] = total.astype(BF16)
+        line = None
         if first:
             eye = iota((lists_here, lists_here), 0) == iota((lists_here, lists_here), 1)
             line = jnp.sum(jnp.where(eye, count, 0.0), axis=0, keepdims=True)
-            if zone_at == 0:
-                count_ref[...] = jnp.where(iota(count_ref.shape, 0) == 2, over, line)
+        if at % 2:
+            put_block(send, at // 2, lists_here, total, line, over)
+        else:
+            if at == 0:
+                own[...] = total
             else:
-                number = line.astype(jnp.int32)
-                high = (number >> 8).astype(F32)
-                low = (number & 255).astype(F32)
-                shape = (16, lists_here)
-                extra = jnp.where(
-                    iota(shape, 0) == 0, high, jnp.where(iota(shape, 0) == 1, low, over)
-                )
-                if width > lists_here:
-                    extra = jnp.concatenate([extra, jnp.zeros((16, width - lists_here), F32)], 1)
-                blocks[zone_at][lists_here:, :] = extra.astype(BF16)
-
-
-def close_kernel(lists_here, width, chunks, zone_count, *refs):
-    fill_ref, own_count = refs[:2]
+                kept[0][(at // 2 - 1) * lists_here : at // 2 * lists_here, :] = total
+            counts.append(line)
+    if first:
+        put_counts(count_ref, counts, over)
+
+
+def put_block(send, place, lists_here, total, line, over):
+    rows = lists_here + (0 if line is None else 16)
+    width = total.shape[1]
+    send[place * rows : place * rows + lists_here, :] = total.astype(BF16)
+    if line is None:
+        return
+    number = line.astype(jnp.int32)
+    high = (number >> 8).astype(F32)
+    low = (number & 255).astype(F32)
+    kind = iota((16, lists_here), 0)
+    extra = jnp.where(kind == 0, high, jnp.where(kind == 1, low, over))
+    if width > lists_here:
+        extra = jnp.concatenate([extra, jnp.zeros((16, width - lists_here), F32)], 1)
+    send[place * rows + lists_here : (place + 1) * rows, :] = extra.astype(BF16)
+
+
+def put_counts(count_ref, counts, over):
+    kind = iota(count_ref.shape, 0)
+    table = jnp.where(kind == count_ref.shape[0] - 1, over, 0.0)
+    for place, line in enumerate(counts):
+        table = jnp.where(kind == place, line, table)
+    count_ref[...] = table
+
+
+def get_counts(got, place, lists_here):
+    rows = lists_here + 16
+    extra = got[place * rows + lists_here : (place + 1) * rows, 0:lists_here].astype(F32)
+    return extra[0:1, :] * 256.0 + extra[1:2, :], extra[2:3, 0:1]
+
+
+def halve_kernel(first, lists_here, blocks, *refs):
+    refs = list(refs)
+    table = refs.pop(0) if first else None
+    got, kept = refs[:2]
+    send = refs[2]
+    rest = refs[3:]
+    rows = lists_here + (16 if first else 0)
+    over = None
+    counts = []
+    for at in range(blocks):
+        line = None
+        if first:
+            line, more = get_counts(got, at, lists_here)
+            line = line + table[at : at + 1, :]
+            over = more + table[table.shape[0] - 1 :, 0:1]
+        if at > 0:
+            total = kept[(at - 1) * lists_here : at * lists_here, :]
+            total = total + got[at * rows : at * rows + lists_here, :].astype(F32)
+            if at % 2:
+                put_block(send, at // 2, lists_here, total, line, over)
+            else:
+                rest[0][(at // 2 - 1) * lists_here : at // 2 * lists_here, :] = total
+        if at % 2 == 0:
+            counts.append(line)
+    if first:
+        put_counts(rest[-1], counts, over)
+
+
+def close_kernel(lists_here, widths, levels, *refs):
+    fill_ref, table = refs[:2]
     refs = refs[2:]
-    drift_ref, count_ref, new_ref = refs[chunks * zone_count :]
-    line = own_count[0:1, :]
-    for at in range(1, zone_count):
-        extra = refs[at][lists_here : lists_here + 16, 0:lists_here].astype(F32)
-        line = line + extra[0:1, :] * 256.0 + extra[1:2, :]
+    chunks = len(widths)
+    drift_ref, count_ref, new_ref = refs[chunks * (1 + levels) :]
+    line, _ = get_counts(refs[levels], 0, lists_here)
+    line = line + table[0:1, :]
     number = line.astype(jnp.int32)
     fill = fill_ref[...]
     count_ref[...] = number
     new_ref[...] = ((fill + number + 127) >> 7) - ((fill + 127) >> 7)
     eye = iota((lists_here, lists_here), 0) == iota((lists_here, lists_here), 1)
     divisor = jnp.sum(jnp.where(eye, jnp.maximum(line, 1.0), 0.0), axis=1, keepdims=True)
-    for chunk in range(chunks):
-        mine = refs[chunk * zone_count : (chunk + 1) * zone_count]
-        total = mine[0][...]
-        for at in range(1, zone_count):
-            total = total + mine[at][0:lists_here, :].astype(F32)
-        drift_ref[:, chunk * width : (chunk + 1) * width] = total / divisor
+    base = 0
+    for chunk, width in enumerate(widths):
+        own, *got = refs[chunk * (1 + levels) : (chunk + 1) * (1 + levels)]
+        total = own[...]
+        for array in got:
+            total = total + array[0:lists_here, :].astype(F32)
+        drift_ref[:, base : base + width] = total / divisor
+        base += width
 
 
 def decode_rows(codes, codebook):
@@ -312,35 +361,40 @@
     return [pl.BlockSpec(memory_space=pltpu.VMEM)] * count
 
 
-def call(kernel, outs, scratch, ins, flops, specs=None):
+def call(kernel, outs, scratch, ins, flops):
     size = sum(a.size * a.dtype.itemsize for a in (*ins, *outs))
     return pl.pallas_call(
         kernel,
         out_shape=outs,
-        in_specs=specs or vmem(len(ins)),
+        in_specs=vmem(len(ins)),
         out_specs=vmem(len(outs)),
         scratch_shapes=scratch,
-        grid=() if specs is None else (1,),
         cost_estimate=pl.CostEstimate(flops=flops, bytes_accessed=size, transcendentals=0),
-        compiler_params=pltpu.CompilerParams(vmem_limit_bytes=56 * 1024 * 1024),
+        compiler_params=pltpu.CompilerParams(vmem_limit_bytes=28 * 1024 * 1024),
     )(*ins)
 
 
 def shape(dims, kind):
     return jax.ShapeDtypeStruct(dims, kind)
+
+
+def cut(feats):
+    units = feats // 128
+    if feats % 128 or units < 3:
+        return [feats]
+    head, tail = CUT[0] * units // 6, CUT[2] * units // 6
+    return [w * 128 for w in (head, units - head - tail, tail) if w]
 
 
 def local(residuals, codes, list_ids, rotation, codebook, list_fill):
     row_count = lax.axis_size("row")
     col_count = lax.axis_size("col")
     vecs, feats = residuals.shape
-    subs = codes.shape[1]
-    dsub = feats // subs
+    dsub = feats // codes.shape[1]
     cents = codebook.shape[0]
     lists_here = list_fill.shape[0]
     zone_count = col_count // 2
-    width = split(feats, CHUNKS)
-    chunks = feats // width
+    widths = cut(feats)
     bound = 3 * vecs // row_count
     slots = up(bound // 2, 16)
 
@@ -349,12 +403,12 @@
 
     ids = list_ids.reshape(1, vecs)
     fill = list_fill.reshape(1, lists_here)
-    extra = tag_rows(slots, width)
     packed = []
     slot = None
-    for chunk in range(chunks):
+    for chunk, width in enumerate(widths):
         first = chunk == 0
-        outs = [shape((slots + (extra if first else 0), width), BF16) for _ in range(row_count)]
+        extra = tag_rows(slots, width) if first else 0
+        outs = [shape((slots + extra, width), BF16) for _ in range(row_count)]
         scratch = [
             pltpu.VMEM((width, vecs), F32),
             pltpu.VMEM((width, cents), F32),
@@ -363,44 +417,41 @@
         if first:
             outs += [shape((8, vecs), jnp.int32)]
         ins = (ids if first else slot, codes.T, residuals, rotation, codebook)
-
-        def all_of(array):
-            return pl.BlockSpec(array.shape, lambda i: (0, 0))
-
-        def columns(array, chunk=chunk):
-            return pl.BlockSpec((array.shape[0], width), lambda i: (0, chunk))
-
-        specs = [*map(all_of, ins[:3]), columns(rotation), columns(codebook)]
+        base = sum(widths[:chunk])
         got = call(
             functools.partial(
-                pack_kernel, first, slots, chunk * width, width, dsub, lists_here, row_count, col_count
+                pack_kernel, first, slots, base, width, dsub, lists_here, row_count, col_count
             ),
             outs,
             scratch,
             ins,
             2 * vecs * width * (feats + row_count * slots),
-            specs,
         )
         packed.append(got[:row_count])
         if first:
             slot = got[row_count]
-    blocks = []
-    key = count = None
-    for chunk in range(chunks):
+    own = []
+    moved = []
+    key = table = None
+    for chunk, width in enumerate(widths):
         first = chunk == 0
+        extra = 16 if first else 0
         mine = packed[chunk]
         got = [mine[0]] + [None] * (row_count - 1)
         for mask in sorted(range(1, row_count), key=lambda m: -bin(m).count("1")):
             got[mask] = trade(mine[mask], "row", row_count, mask)
         other = [trade(got[0], "col", col_count, 1)]
         other += [trade(array, "col", col_count, 1) for array in got[1:]]
-        outs = [shape((lists_here, width), F32)]
-        outs += [
-            shape((lists_here + (16 if first else 0), width), BF16) for _ in range(zone_count - 1)
+        blocks = zone_count // 2
+        outs = [
+            shape((lists_here, width), F32),
+            shape((blocks * (lists_here + extra), width), BF16),
         ]
+        if blocks > 1:
+            outs += [shape(((blocks - 1) * lists_here, width), F32)]
         ins = [*got, *other]
         if first:
-            outs += [shape((8, lists_here), F32), shape((2 * row_count, slots), jnp.int32)]
+            outs += [shape((16, lists_here), F32), shape((2 * row_count, slots), jnp.int32)]
         else:
             ins = [key, *ins]
         sums = call(
@@ -411,30 +462,51 @@
             2 * zone_count * lists_here * 2 * row_count * slots * width,
         )
         if first:
-            count, key = sums[zone_count:]
-        blocks.append(sums[:zone_count])
+            table, key = sums[-2:]
+        own.append(sums[0])
+        moved.append(sums[1 : 3 if blocks > 1 else 2])
     landed = []
-    for chunk in range(chunks):
-        mine = blocks[chunk]
-        landed.append(mine[0])
-        got = [None] * zone_count
-        for mask in sorted(range(1, zone_count), key=lambda m: -m):
-            got[mask] = trade(mine[mask], "col", col_count, 2 * mask)
-        landed += got[1:]
-    over = count[2, 0]
-    for array in landed[1:zone_count]:
-        over = over + array[lists_here + 2, 0].astype(F32)
+    levels = 0
+    for chunk, width in enumerate(widths):
+        first = chunk == 0
+        extra = 16 if first else 0
+        send, *kept = moved[chunk]
+        landed.append(own[chunk])
+        levels = 0
+        blocks = zone_count // 2
+        while blocks:
+            got = trade(send, "col", col_count, 2 << levels)
+            landed.append(got)
+            levels += 1
+            half = blocks // 2
+            if half:
+                outs = [shape((half * (lists_here + extra), width), BF16)]
+                if half > 1:
+                    outs += [shape(((half - 1) * lists_here, width), F32)]
+                if first:
+                    outs += [shape((16, lists_here), F32)]
+                send, *kept = call(
+                    functools.partial(halve_kernel, first, lists_here, blocks),
+                    outs,
+                    [],
+                    [*([table] if first else []), got, *kept],
+                    blocks * lists_here * width,
+                )
+                if first:
+                    table = kept.pop()
+            blocks = half
+    over = table[15, 0] + landed[levels][lists_here + 2, 0].astype(F32)
 
     def close(*arrays):
         drift, counts, new_blocks = call(
-            functools.partial(close_kernel, lists_here, width, chunks, zone_count),
+            functools.partial(close_kernel, lists_here, widths, levels),
             [
                 shape((lists_here, feats), F32),
                 shape((1, lists_here), jnp.int32),
                 shape((1, lists_here), jnp.int32),
             ],
             [],
-            [fill, count, *arrays],
+            [fill, table, *arrays],
             lists_here * feats * zone_count,
         )
         return drift, counts.reshape(-1), new_blocks.reshape(-1)

time: 95.3 us -> 79.3 us (0.83)
  Pallas kernels: 30.3 us -> 15.2 us
  waiting for transfers between devices: 25.2 us -> 34.7 us
  starting transfers between devices: 33.1 us -> 26.1 us
  local copies, waits for them, and re-layouts: 2.56 us -> 1.06 us
  between operations: 3.5 us -> 2.12 us
    pallas_call x7 -> x10, Pallas kernels: 30.3 us -> 15.2 us  [call(): pl.pallas_call(kernel, out_shape=outs, in_specs=vmem(len(ins)), out_specs...]
    ppermute x30 -> x27, waiting for transfers between devices: 25.2 us -> 34.7 us  [trade(): return lax.ppermute(array, axis, [(i, i ^ mask) for i in range(size)])]
    ppermute x30 -> x27, starting transfers between devices: 33.1 us -> 26.1 us  [trade(): return lax.ppermute(array, axis, [(i, i ^ mask) for i in range(size)])]
    slice x4 -> x2, local copies, waits for them, and re-layouts: 2.06 us -> 1.03 us  [local(): over = table[15, 0] + landed[levels][lists_here + 2, 0].astype(F32)]
  transfers between devices with their start and end apart: 30 -> 27, of which waited for: 9 -> 11; matrix products, arithmetic and copies ran while one was open for 2% -> 1% of each run, Pallas kernels for 18% -> 10%
where the time goes in v3:
time: 79.3 us; the launch traced here: 79.1 us
  waiting for transfers between devices  34.7 us (44%)
  starting transfers between devices  26.1 us (33%)
  Pallas kernels  15.2 us (19%)
  between operations  2.12 us (3%)
  local copies, waits for them, and re-layouts  1.06 us (1%)
    ppermute x27, waiting for transfers between devices, trade(): return lax.ppermute(array, axis, [(i, i ^ mask) for i in range(size)])  34.7 us
    ppermute x27, starting transfers between devices, trade(): return lax.ppermute(array, axis, [(i, i ^ mask) for i in range(size)])  26.1 us
    pallas_call x10, Pallas kernels, call(): pl.pallas_call(kernel, out_shape=outs, in_specs=vmem(len(ins)), out_specs...  15.2 us
  transfers between devices with their start and end apart: 27, of which 11 were waited for; matrix products, arithmetic and copies ran while one was open for 1% of the time, Pallas kernels for 10%

profile of v3, /device:TPU:0, one launch (start us, length us, event | category | flops | bytes accessed | tf_op | source)
XLA Modules:
  0.0 79.1 jit_solution(5197742190477927452)
XLA Ops:
  0.7 4.8 %shard_map.89 = (bf16[400,256]{1,0:T(8,128)(2,1)S(1)}, bf16[400,256]{1,0:T(8,128)(2,1)S(1)}, bf16[400,256]{1,0:T(8,128)(2,1)S(1)}, bf16[400,256]{1,0:T(8,128)(2,1)S(1)}, s32[8,1024]{1,0:T(8,128)S(1)}) custom-call(s32[1,1024]{1,0:T(1,128)} %bitcast.39, s32[64,1024]{1,0:T(8,128)} %bitcast.36, bf16[1024,768]{1,0:T(8,128)(2,1)} %refs_2_.5, ...), custom_call_target="tpu_custom_call" | custom-call | flops 1207959552 | bytes 4263936 | tf_op jit(solution)/shard_map/pallas_call | solution.py:366
  5.5 1.7 %shard_map.92 = (bf16[384,256]{1,0:T(8,128)(2,1)S(1)}, bf16[384,256]{1,0:T(8,128)(2,1)S(1)}, bf16[384,256]{1,0:T(8,128)(2,1)S(1)}, bf16[384,256]{1,0:T(8,128)(2,1)S(1)}) custom-call(s32[8,1024]{1,0:T(8,128)S(1)} %get-tuple-element.117.refs_0_, s32[64,1024]{1,0:T(8,128)S(1)} %bitcast.37, bf16[1024,768]{1,0:T(8,128)(2,1)S(1)} %copy-done.5, ...), custom_call_target="tpu_custom_call" | custom-call | flops 1207959552 | bytes 4227072 | tf_op jit(solution)/shard_map/pallas_call | solution.py:366
  7.2 3.0 %collective-permute-start.9 = (bf16[384,256]{1,0:T(8,128)(2,1)S(1)}, bf16[384,256]{1,0:T(8,128)(2,1)S(1)}, u32[]{:S(2)}, u32[]{:S(2)}) collective-permute-start(bf16[384,256]{1,0:T(8,128)(2,1)S(1)} %get-tuple-element.119), channel_id=1, source_target_pairs={{0,8},{8,0},{16,24},{24,16},{1,9},{9,1},{17,25},{25,17},{2,10},{10... | collective-permute-start | bytes 589832 | tf_op jit(solution)/shard_map/ppermute | solution.py:402
  10.2 1.5 %collective-permute-start.10 = (bf16[384,256]{1,0:T(8,128)(2,1)S(1)}, bf16[384,256]{1,0:T(8,128)(2,1)S(1)}, u32[]{:S(2)}, u32[]{:S(2)}) collective-permute-start(bf16[384,256]{1,0:T(8,128)(2,1)S(1)} %get-tuple-element.120), channel_id=1, source_target_pairs={{0,16},{8,24},{16,0},{24,8},{1,17},{9,25},{17,1},{25,9},{2,18},{10... | collective-permute-start | bytes 589832 | tf_op jit(solution)/shard_map/ppermute | solution.py:402
  11.8 1.7 %shard_map.95 = (bf16[384,256]{1,0:T(8,128)(2,1)S(1)}, bf16[384,256]{1,0:T(8,128)(2,1)S(1)}, bf16[384,256]{1,0:T(8,128)(2,1)S(1)}, bf16[384,256]{1,0:T(8,128)(2,1)S(1)}) custom-call(s32[8,1024]{1,0:T(8,128)S(1)} %get-tuple-element.117.refs_0_, s32[64,1024]{1,0:T(8,128)S(1)} %bitcast.38, bf16[1024,768]{1,0:T(8,128)(2,1)S(1)} %copy-done.5, ...), custom_call_target="tpu_custom_call" | custom-call | flops 1207959552 | bytes 4227072 | tf_op jit(solution)/shard_map/pallas_call | solution.py:366
  13.5 2.0 %collective-permute-start.18 = (bf16[384,256]{1,0:T(8,128)(2,1)S(1)}, bf16[384,256]{1,0:T(8,128)(2,1)S(1)}, u32[]{:S(2)}, u32[]{:S(2)}) collective-permute-start(bf16[384,256]{1,0:T(8,128)(2,1)S(1)} %get-tuple-element.126), channel_id=1, source_target_pairs={{0,8},{8,0},{16,24},{24,16},{1,9},{9,1},{17,25},{25,17},{2,10},{10... | collective-permute-start | bytes 589832 | tf_op jit(solution)/shard_map/ppermute | solution.py:402
  16.0 2.0 %collective-permute-start.19 = (bf16[384,256]{1,0:T(8,128)(2,1)S(1)}, bf16[384,256]{1,0:T(8,128)(2,1)S(1)}, u32[]{:S(2)}, u32[]{:S(2)}) collective-permute-start(bf16[384,256]{1,0:T(8,128)(2,1)S(1)} %get-tuple-element.127), channel_id=1, source_target_pairs={{0,16},{8,24},{16,0},{24,8},{1,17},{9,25},{17,1},{25,9},{2,18},{10... | collective-permute-start | bytes 589832 | tf_op jit(solution)/shard_map/ppermute | solution.py:402
  18.0 3.2 %collective-permute-done.10.refs_3_ = bf16[384,256]{1,0:T(8,128)(2,1)S(1)} collective-permute-done((bf16[384,256]{1,0:T(8,128)(2,1)S(1)}, bf16[384,256]{1,0:T(8,128)(2,1)S(1)}, u32[]{:S(2)}, u32[]{:S(2)}) %collective-permute-start.10) | collective-permute-done | bytes 196640 | tf_op jit(solution)/shard_map/ppermute | solution.py:402
  21.8 3.4 %collective-permute-start = (bf16[400,256]{1,0:T(8,128)(2,1)S(1)}, bf16[400,256]{1,0:T(8,128)(2,1)S(1)}, u32[]{:S(2)}, u32[]{:S(2)}) collective-permute-start(bf16[400,256]{1,0:T(8,128)(2,1)S(1)} %get-tuple-element.107), channel_id=1, source_target_pairs={{0,8},{8,0},{16,24},{24,16},{1,9},{9,1},{17,25},{25,17},{2,10},{10... | collective-permute-start | bytes 614408 | tf_op jit(solution)/shard_map/ppermute | solution.py:402
  25.2 2.2 %collective-permute-start.2 = (bf16[400,256]{1,0:T(8,128)(2,1)S(1)}, bf16[400,256]{1,0:T(8,128)(2,1)S(1)}, u32[]{:S(2)}, u32[]{:S(2)}) collective-permute-start(bf16[400,256]{1,0:T(8,128)(2,1)S(1)} %get-tuple-element.109), channel_id=1, source_target_pairs={{0,24},{8,16},{16,8},{24,0},{1,25},{9,17},{17,9},{25,1},{2,26},{10... | collective-permute-start | bytes 614408 | tf_op jit(solution)/shard_map/ppermute | solution.py:402
  27.4 3.3 %collective-permute-done.19.refs_3_ = bf16[384,256]{1,0:T(8,128)(2,1)S(1)} collective-permute-done((bf16[384,256]{1,0:T(8,128)(2,1)S(1)}, bf16[384,256]{1,0:T(8,128)(2,1)S(1)}, u32[]{:S(2)}, u32[]{:S(2)}) %collective-permute-start.19) | collective-permute-done | bytes 196640 | tf_op jit(solution)/shard_map/ppermute | solution.py:402
  31.2 3.3 %collective-permute-done.refs_1_ = bf16[400,256]{1,0:T(8,128)(2,1)S(1)} collective-permute-done((bf16[400,256]{1,0:T(8,128)(2,1)S(1)}, bf16[400,256]{1,0:T(8,128)(2,1)S(1)}, u32[]{:S(2)}, u32[]{:S(2)}) %collective-permute-start) | collective-permute-done | bytes 204832 | tf_op jit(solution)/shard_map/ppermute | solution.py:402
  34.5 3.5 %collective-permute-done.1.refs_2_ = bf16[400,256]{1,0:T(8,128)(2,1)S(1)} collective-permute-done((bf16[400,256]{1,0:T(8,128)(2,1)S(1)}, bf16[400,256]{1,0:T(8,128)(2,1)S(1)}, u32[]{:S(2)}, u32[]{:S(2)}) %collective-permute-start.1) | collective-permute-done | bytes 204832 | tf_op jit(solution)/shard_map/ppermute | solution.py:402
  41.1 2.1 %shard_map.90 = (f32[256,256]{1,0:T(8,128)S(1)}, bf16[544,256]{1,0:T(8,128)(2,1)S(1)}, f32[256,256]{1,0:T(8,128)S(1)}, f32[16,256]{1,0:T(8,128)S(1)}, s32[8,384]{1,0:T(8,128)S(1)}) custom-call(bf16[400,256]{1,0:T(8,128)(2,1)S(1)} %get-tuple-element.106.refs_0_, bf16[400,256]{1,0:T(8,128)(2,1)S(1)} %collective-permute-done.refs_1_, ...), custom_call_target="tpu_custom_call" | custom-call | flops 1610612736 | bytes 2469888 | tf_op jit(solution)/shard_map/pallas_call | solution.py:366
  43.2 1.6 %collective-permute-start.7 = (bf16[544,256]{1,0:T(8,128)(2,1)S(1)}, bf16[544,256]{1,0:T(8,128)(2,1)S(1)}, u32[]{:S(2)}, u32[]{:S(2)}) collective-permute-start(bf16[544,256]{1,0:T(8,128)(2,1)S(1)} %get-tuple-element.111), channel_id=1, source_target_pairs={{0,2},{1,3},{2,0},{3,1},{4,6},{5,7},{6,4},{7,5},{8,10},{9,11},{10,... | collective-permute-start | bytes 835592 | tf_op jit(solution)/shard_map/ppermute | solution.py:402
  44.9 1.8 %shard_map.93 = (f32[256,256]{1,0:T(8,128)S(1)}, bf16[512,256]{1,0:T(8,128)(2,1)S(1)}, f32[256,256]{1,0:T(8,128)S(1)}) custom-call(s32[8,384]{1,0:T(8,128)S(1)} %get-tuple-element.116.refs_0_, bf16[384,256]{1,0:T(8,128)(2,1)S(1)} %get-tuple-element.118.refs_1_, bf16[384,256]{1,0:T(8,128)(2,1)S(1)} %collective-permute-done.9.refs_2_, ...), custom_call_target="tpu_custom_call" | custom-call | flops 1610612736 | bytes 2371584 | tf_op jit(solution)/shard_map/pallas_call | solution.py:366
  47.2 2.0 %shard_map.96 = (f32[256,256]{1,0:T(8,128)S(1)}, bf16[512,256]{1,0:T(8,128)(2,1)S(1)}, f32[256,256]{1,0:T(8,128)S(1)}) custom-call(s32[8,384]{1,0:T(8,128)S(1)} %get-tuple-element.116.refs_0_, bf16[384,256]{1,0:T(8,128)(2,1)S(1)} %get-tuple-element.125.refs_1_, bf16[384,256]{1,0:T(8,128)(2,1)S(1)} %collective-permute-done.18.refs_2_, ...), custom_call_target="tpu_custom_call" | custom-call | flops 1610612736 | bytes 2371584 | tf_op jit(solution)/shard_map/pallas_call | solution.py:366
  49.2 1.6 %collective-permute-start.25 = (bf16[512,256]{1,0:T(8,128)(2,1)S(1)}, bf16[512,256]{1,0:T(8,128)(2,1)S(1)}, u32[]{:S(2)}, u32[]{:S(2)}) collective-permute-start(bf16[512,256]{1,0:T(8,128)(2,1)S(1)} %get-tuple-element.130), channel_id=1, source_target_pairs={{0,2},{1,3},{2,0},{3,1},{4,6},{5,7},{6,4},{7,5},{8,10},{9,11},{10,... | collective-permute-start | bytes 786440 | tf_op jit(solution)/shard_map/ppermute | solution.py:402
  50.8 2.0 %collective-permute-done.7.refs_1_ = bf16[544,256]{1,0:T(8,128)(2,1)S(1)} collective-permute-done((bf16[544,256]{1,0:T(8,128)(2,1)S(1)}, bf16[544,256]{1,0:T(8,128)(2,1)S(1)}, u32[]{:S(2)}, u32[]{:S(2)}) %collective-permute-start.7) | collective-permute-done | bytes 278560 | tf_op jit(solution)/shard_map/ppermute | solution.py:402
  52.9 2.7 %collective-permute-start.8 = (bf16[272,256]{1,0:T(8,128)(2,1)S(1)}, bf16[272,256]{1,0:T(8,128)(2,1)S(1)}, u32[]{:S(2)}, u32[]{:S(2)}) collective-permute-start(bf16[272,256]{1,0:T(8,128)(2,1)S(1)} %get-tuple-element.114), channel_id=1, source_target_pairs={{0,4},{1,5},{2,6},{3,7},{4,0},{5,1},{6,2},{7,3},{8,12},{9,13},{10,... | collective-permute-start | bytes 417800 | tf_op jit(solution)/shard_map/ppermute | solution.py:402
  55.5 5.9 %collective-permute-done.16.refs_0_ = bf16[512,256]{1,0:T(8,128)(2,1)S(1)} collective-permute-done((bf16[512,256]{1,0:T(8,128)(2,1)S(1)}, bf16[512,256]{1,0:T(8,128)(2,1)S(1)}, u32[]{:S(2)}, u32[]{:S(2)}) %collective-permute-start.16) | collective-permute-done | bytes 262176 | tf_op jit(solution)/shard_map/ppermute | solution.py:402
  61.4 1.8 %collective-permute-start.17 = (bf16[256,256]{1,0:T(8,128)(2,1)S(1)}, bf16[256,256]{1,0:T(8,128)(2,1)S(1)}, u32[]{:S(2)}, u32[]{:S(2)}) collective-permute-start(bf16[256,256]{1,0:T(8,128)(2,1)S(1)} %shard_map.94), channel_id=1, source_target_pairs={{0,4},{1,5},{2,6},{3,7},{4,0},{5,1},{6,2},{7,3},{8,12},{9,13},{10,... | collective-permute-start | bytes 393224 | tf_op jit(solution)/shard_map/ppermute | solution.py:402
  63.2 4.5 %collective-permute-done.25.refs_0_ = bf16[512,256]{1,0:T(8,128)(2,1)S(1)} collective-permute-done((bf16[512,256]{1,0:T(8,128)(2,1)S(1)}, bf16[512,256]{1,0:T(8,128)(2,1)S(1)}, u32[]{:S(2)}, u32[]{:S(2)}) %collective-permute-start.25) | collective-permute-done | bytes 262176 | tf_op jit(solution)/shard_map/ppermute | solution.py:402
  70.6 6.0 %collective-permute-done.17 = bf16[256,256]{1,0:T(8,128)(2,1)S(1)} collective-permute-done((bf16[256,256]{1,0:T(8,128)(2,1)S(1)}, bf16[256,256]{1,0:T(8,128)(2,1)S(1)}, u32[]{:S(2)}, u32[]{:S(2)}) %collective-permute-start.17) | collective-permute-done | bytes 131104 | tf_op jit(solution)/shard_map/ppermute | solution.py:402
  (55 shorter events, 10.4 us)
Async XLA Ops:
  7.2 8.8 %collective-permute-start.9 = (bf16[384,256]{1,0:T(8,128)(2,1)S(1)}, bf16[384,256]{1,0:T(8,128)(2,1)S(1)}, u32[]{:S(2)}, u32[]{:S(2)}) collective-permute-start(bf16[384,256]{1,0:T(8,128)(2,1)S(1)} %get-tuple-element.119), channel_id=1, source_target_pairs={{0,8},{8,0},{16,24},{24,16},{1,9},{9,1},{17,25},{25,17},{2,10},{10... | collective-permute-start | bytes 589832 | tf_op jit(solution)/shard_map/ppermute | solution.py:402
  10.2 11.0 %collective-permute-start.10 = (bf16[384,256]{1,0:T(8,128)(2,1)S(1)}, bf16[384,256]{1,0:T(8,128)(2,1)S(1)}, u32[]{:S(2)}, u32[]{:S(2)}) collective-permute-start(bf16[384,256]{1,0:T(8,128)(2,1)S(1)} %get-tuple-element.120), channel_id=1, source_target_pairs={{0,16},{8,24},{16,0},{24,8},{1,17},{9,25},{17,1},{25,9},{2,18},{10... | collective-permute-start | bytes 589832 | tf_op jit(solution)/shard_map/ppermute | solution.py:402
  11.7 10.1 %collective-permute-start.11 = (bf16[384,256]{1,0:T(8,128)(2,1)S(1)}, bf16[384,256]{1,0:T(8,128)(2,1)S(1)}, u32[]{:S(2)}, u32[]{:S(2)}) collective-permute-start(bf16[384,256]{1,0:T(8,128)(2,1)S(1)} %get-tuple-element.121), channel_id=1, source_target_pairs={{0,24},{8,16},{16,8},{24,0},{1,25},{9,17},{17,9},{25,1},{2,26},{10... | collective-permute-start | bytes 589832 | tf_op jit(solution)/shard_map/ppermute | solution.py:402
  11.8 13.4 %collective-permute-start.12 = (bf16[384,256]{1,0:T(8,128)(2,1)S(1)}, bf16[384,256]{1,0:T(8,128)(2,1)S(1)}, u32[]{:S(2)}, u32[]{:S(2)}) collective-permute-start(bf16[384,256]{1,0:T(8,128)(2,1)S(1)} %get-tuple-element.118.refs_1_), channel_id=1, source_target_pairs={{0,1},{1,0},{2,3},{3,2},{4,5},{5,4},{6,7},{7,6},{8,9},{9,8},{10,11... | collective-permute-start | bytes 589832 | tf_op jit(solution)/shard_map/ppermute | solution.py:402
  13.5 11.7 %collective-permute-start.18 = (bf16[384,256]{1,0:T(8,128)(2,1)S(1)}, bf16[384,256]{1,0:T(8,128)(2,1)S(1)}, u32[]{:S(2)}, u32[]{:S(2)}) collective-permute-start(bf16[384,256]{1,0:T(8,128)(2,1)S(1)} %get-tuple-element.126), channel_id=1, source_target_pairs={{0,8},{8,0},{16,24},{24,16},{1,9},{9,1},{17,25},{25,17},{2,10},{10... | collective-permute-start | bytes 589832 | tf_op jit(solution)/shard_map/ppermute | solution.py:402
  16.0 14.7 %collective-permute-start.19 = (bf16[384,256]{1,0:T(8,128)(2,1)S(1)}, bf16[384,256]{1,0:T(8,128)(2,1)S(1)}, u32[]{:S(2)}, u32[]{:S(2)}) collective-permute-start(bf16[384,256]{1,0:T(8,128)(2,1)S(1)} %get-tuple-element.127), channel_id=1, source_target_pairs={{0,16},{8,24},{16,0},{24,8},{1,17},{9,25},{17,1},{25,9},{2,18},{10... | collective-permute-start | bytes 589832 | tf_op jit(solution)/shard_map/ppermute | solution.py:402
  21.2 9.4 %collective-permute-start.20 = (bf16[384,256]{1,0:T(8,128)(2,1)S(1)}, bf16[384,256]{1,0:T(8,128)(2,1)S(1)}, u32[]{:S(2)}, u32[]{:S(2)}) collective-permute-start(bf16[384,256]{1,0:T(8,128)(2,1)S(1)} %get-tuple-element.128), channel_id=1, source_target_pairs={{0,24},{8,16},{16,8},{24,0},{1,25},{9,17},{17,9},{25,1},{2,26},{10... | collective-permute-start | bytes 589832 | tf_op jit(solution)/shard_map/ppermute | solution.py:402
  21.8 12.6 %collective-permute-start = (bf16[400,256]{1,0:T(8,128)(2,1)S(1)}, bf16[400,256]{1,0:T(8,128)(2,1)S(1)}, u32[]{:S(2)}, u32[]{:S(2)}) collective-permute-start(bf16[400,256]{1,0:T(8,128)(2,1)S(1)} %get-tuple-element.107), channel_id=1, source_target_pairs={{0,8},{8,0},{16,24},{24,16},{1,9},{9,1},{17,25},{25,17},{2,10},{10... | collective-permute-start | bytes 614408 | tf_op jit(solution)/shard_map/ppermute | solution.py:402
  25.2 12.8 %collective-permute-start.1 = (bf16[400,256]{1,0:T(8,128)(2,1)S(1)}, bf16[400,256]{1,0:T(8,128)(2,1)S(1)}, u32[]{:S(2)}, u32[]{:S(2)}) collective-permute-start(bf16[400,256]{1,0:T(8,128)(2,1)S(1)} %get-tuple-element.108), channel_id=1, source_target_pairs={{0,16},{8,24},{16,0},{24,8},{1,17},{9,25},{17,1},{25,9},{2,18},{10... | collective-permute-start | bytes 614408 | tf_op jit(solution)/shard_map/ppermute | solution.py:402
  25.2 12.8 %collective-permute-start.2 = (bf16[400,256]{1,0:T(8,128)(2,1)S(1)}, bf16[400,256]{1,0:T(8,128)(2,1)S(1)}, u32[]{:S(2)}, u32[]{:S(2)}) collective-permute-start(bf16[400,256]{1,0:T(8,128)(2,1)S(1)} %get-tuple-element.109), channel_id=1, source_target_pairs={{0,24},{8,16},{16,8},{24,0},{1,25},{9,17},{17,9},{25,1},{2,26},{10... | collective-permute-start | bytes 614408 | tf_op jit(solution)/shard_map/ppermute | solution.py:402
  30.7 7.8 %collective-permute-start.3 = (bf16[400,256]{1,0:T(8,128)(2,1)S(1)}, bf16[400,256]{1,0:T(8,128)(2,1)S(1)}, u32[]{:S(2)}, u32[]{:S(2)}) collective-permute-start(bf16[400,256]{1,0:T(8,128)(2,1)S(1)} %get-tuple-element.106.refs_0_), channel_id=1, source_target_pairs={{0,1},{1,0},{2,3},{3,2},{4,5},{5,4},{6,7},{7,6},{8,9},{9,8},{10,11... | collective-permute-start | bytes 614408 | tf_op jit(solution)/shard_map/ppermute | solution.py:402
  30.7 7.9 %collective-permute-start.13 = (bf16[384,256]{1,0:T(8,128)(2,1)S(1)}, bf16[384,256]{1,0:T(8,128)(2,1)S(1)}, u32[]{:S(2)}, u32[]{:S(2)}) collective-permute-start(bf16[384,256]{1,0:T(8,128)(2,1)S(1)} %collective-permute-done.9.refs_2_), channel_id=1, source_target_pairs={{0,1},{1,0},{2,3},{3,2},{4,5},{5,4},{6,7},{7,6},{8,9},{9,8},{10,11... | collective-permute-start | bytes 589832 | tf_op jit(solution)/shard_map/ppermute | solution.py:402
  34.5 5.8 %collective-permute-start.4 = (bf16[400,256]{1,0:T(8,128)(2,1)S(1)}, bf16[400,256]{1,0:T(8,128)(2,1)S(1)}, u32[]{:S(2)}, u32[]{:S(2)}) collective-permute-start(bf16[400,256]{1,0:T(8,128)(2,1)S(1)} %collective-permute-done.refs_1_), channel_id=1, source_target_pairs={{0,1},{1,0},{2,3},{3,2},{4,5},{5,4},{6,7},{7,6},{8,9},{9,8},{10,11... | collective-permute-start | bytes 614408 | tf_op jit(solution)/shard_map/ppermute | solution.py:402
  38.6 4.6 %collective-permute-start.15 = (bf16[384,256]{1,0:T(8,128)(2,1)S(1)}, bf16[384,256]{1,0:T(8,128)(2,1)S(1)}, u32[]{:S(2)}, u32[]{:S(2)}) collective-permute-start(bf16[384,256]{1,0:T(8,128)(2,1)S(1)} %collective-permute-done.11.refs_4_), channel_id=1, source_target_pairs={{0,1},{1,0},{2,3},{3,2},{4,5},{5,4},{6,7},{7,6},{8,9},{9,8},{10,11... | collective-permute-start | bytes 589832 | tf_op jit(solution)/shard_map/ppermute | solution.py:402
  40.0 6.6 %collective-permute-start.21 = (bf16[384,256]{1,0:T(8,128)(2,1)S(1)}, bf16[384,256]{1,0:T(8,128)(2,1)S(1)}, u32[]{:S(2)}, u32[]{:S(2)}) collective-permute-start(bf16[384,256]{1,0:T(8,128)(2,1)S(1)} %get-tuple-element.125.refs_1_), channel_id=1, source_target_pairs={{0,1},{1,0},{2,3},{3,2},{4,5},{5,4},{6,7},{7,6},{8,9},{9,8},{10,11... | collective-permute-start | bytes 589832 | tf_op jit(solution)/shard_map/ppermute | solution.py:402
  40.2 7.0 %collective-permute-start.22 = (bf16[384,256]{1,0:T(8,128)(2,1)S(1)}, bf16[384,256]{1,0:T(8,128)(2,1)S(1)}, u32[]{:S(2)}, u32[]{:S(2)}) collective-permute-start(bf16[384,256]{1,0:T(8,128)(2,1)S(1)} %collective-permute-done.18.refs_2_), channel_id=1, source_target_pairs={{0,1},{1,0},{2,3},{3,2},{4,5},{5,4},{6,7},{7,6},{8,9},{9,8},{10,11... | collective-permute-start | bytes 589832 | tf_op jit(solution)/shard_map/ppermute | solution.py:402
  40.5 6.7 %collective-permute-start.23 = (bf16[384,256]{1,0:T(8,128)(2,1)S(1)}, bf16[384,256]{1,0:T(8,128)(2,1)S(1)}, u32[]{:S(2)}, u32[]{:S(2)}) collective-permute-start(bf16[384,256]{1,0:T(8,128)(2,1)S(1)} %collective-permute-done.19.refs_3_), channel_id=1, source_target_pairs={{0,1},{1,0},{2,3},{3,2},{4,5},{5,4},{6,7},{7,6},{8,9},{9,8},{10,11... | collective-permute-start | bytes 589832 | tf_op jit(solution)/shard_map/ppermute | solution.py:402
  40.8 6.4 %collective-permute-start.24 = (bf16[384,256]{1,0:T(8,128)(2,1)S(1)}, bf16[384,256]{1,0:T(8,128)(2,1)S(1)}, u32[]{:S(2)}, u32[]{:S(2)}) collective-permute-start(bf16[384,256]{1,0:T(8,128)(2,1)S(1)} %collective-permute-done.20.refs_4_), channel_id=1, source_target_pairs={{0,1},{1,0},{2,3},{3,2},{4,5},{5,4},{6,7},{7,6},{8,9},{9,8},{10,11... | collective-permute-start | bytes 589832 | tf_op jit(solution)/shard_map/ppermute | solution.py:402
  43.2 9.6 %collective-permute-start.7 = (bf16[544,256]{1,0:T(8,128)(2,1)S(1)}, bf16[544,256]{1,0:T(8,128)(2,1)S(1)}, u32[]{:S(2)}, u32[]{:S(2)}) collective-permute-start(bf16[544,256]{1,0:T(8,128)(2,1)S(1)} %get-tuple-element.111), channel_id=1, source_target_pairs={{0,2},{1,3},{2,0},{3,1},{4,6},{5,7},{6,4},{7,5},{8,10},{9,11},{10,... | collective-permute-start | bytes 835592 | tf_op jit(solution)/shard_map/ppermute | solution.py:402
  46.7 14.7 %collective-permute-start.16 = (bf16[512,256]{1,0:T(8,128)(2,1)S(1)}, bf16[512,256]{1,0:T(8,128)(2,1)S(1)}, u32[]{:S(2)}, u32[]{:S(2)}) collective-permute-start(bf16[512,256]{1,0:T(8,128)(2,1)S(1)} %get-tuple-element.123), channel_id=1, source_target_pairs={{0,2},{1,3},{2,0},{3,1},{4,6},{5,7},{6,4},{7,5},{8,10},{9,11},{10,... | collective-permute-start | bytes 786440 | tf_op jit(solution)/shard_map/ppermute | solution.py:402
  49.2 18.5 %collective-permute-start.25 = (bf16[512,256]{1,0:T(8,128)(2,1)S(1)}, bf16[512,256]{1,0:T(8,128)(2,1)S(1)}, u32[]{:S(2)}, u32[]{:S(2)}) collective-permute-start(bf16[512,256]{1,0:T(8,128)(2,1)S(1)} %get-tuple-element.130), channel_id=1, source_target_pairs={{0,2},{1,3},{2,0},{3,1},{4,6},{5,7},{6,4},{7,5},{8,10},{9,11},{10,... | collective-permute-start | bytes 786440 | tf_op jit(solution)/shard_map/ppermute | solution.py:402
  52.9 15.9 %collective-permute-start.8 = (bf16[272,256]{1,0:T(8,128)(2,1)S(1)}, bf16[272,256]{1,0:T(8,128)(2,1)S(1)}, u32[]{:S(2)}, u32[]{:S(2)}) collective-permute-start(bf16[272,256]{1,0:T(8,128)(2,1)S(1)} %get-tuple-element.114), channel_id=1, source_target_pairs={{0,4},{1,5},{2,6},{3,7},{4,0},{5,1},{6,2},{7,3},{8,12},{9,13},{10,... | collective-permute-start | bytes 417800 | tf_op jit(solution)/shard_map/ppermute | solution.py:402
  61.4 15.2 %collective-permute-start.17 = (bf16[256,256]{1,0:T(8,128)(2,1)S(1)}, bf16[256,256]{1,0:T(8,128)(2,1)S(1)}, u32[]{:S(2)}, u32[]{:S(2)}) collective-permute-start(bf16[256,256]{1,0:T(8,128)(2,1)S(1)} %shard_map.94), channel_id=1, source_target_pairs={{0,4},{1,5},{2,6},{3,7},{4,0},{5,1},{6,2},{7,3},{8,12},{9,13},{10,... | collective-permute-start | bytes 393224 | tf_op jit(solution)/shard_map/ppermute | solution.py:402
  67.8 10.3 %collective-permute-start.26 = (bf16[256,256]{1,0:T(8,128)(2,1)S(1)}, bf16[256,256]{1,0:T(8,128)(2,1)S(1)}, u32[]{:S(2)}, u32[]{:S(2)}) collective-permute-start(bf16[256,256]{1,0:T(8,128)(2,1)S(1)} %shard_map.97), channel_id=1, source_target_pairs={{0,4},{1,5},{2,6},{3,7},{4,0},{5,1},{6,2},{7,3},{8,12},{9,13},{10,... | collective-permute-start | bytes 393224 | tf_op jit(solution)/shard_map/ppermute | solution.py:402
  (9 other events, 88.9 us)
